TPU v7x, 128 devices: a whole 4x4x4 slice. The times are simulated.
128 devices in a mesh: run: 16 (over z, y_hi, core), strip: 8 (over y_lo, x).
Axes of the slice: x: 4, y: 4 (y_hi: 2, y_lo: 2; y = y_hi * 2 + y_lo), z: 4, core: 2. Of those that a mesh axis runs over, the one named last changes fastest.
Arguments:
- base_field: float32 [512, 8, 256], P('strip'), may hold values from -3 to 3
- material_map: int32 [512, 8, 256], P('strip'), may hold values from 0 to 3
- param_levels: float32 [6, 8], replicated, may hold values from 0.2 to 1
- param_index: int32 [64, 6], replicated, may hold values from 0 to 7
- w_input: float32 [8, 512], replicated, may hold values from -2 to 2
- w_output: bfloat16 [512, 512, 2048], P(None, 'strip', 'run'), may hold values from -0.375 to 0.375
Outputs:
- grad_output: bfloat16 [512, 512, 2048], P(None, 'strip', 'run')
- grad_input: float32 [8, 512], P(None, ('run', 'strip'))
All inputs are finite; a program needn't handle non-finite values.
Results may differ from a plain program's by a relative error of at most 0.0025.
Values may be sent and summed in bfloat16 or wider, within the bound.
A program may use at most 128 MiB of HBM per device.

v0:
```python
import jax
import jax.numpy as jnp
from jax import lax
from jax.sharding import PartitionSpec as P

STEPS = 4


time_step = 0.08


def padded_2(value, sides, width):
    for axis, dim in sides:
        size, length = (lax.axis_size(axis), value.shape[dim])
        up = [(i, (i + 1) % size) for i in range(size - 1)]
        down = [(j, i) for i, j in up]
        last = lax.slice_in_dim(value, length - width, length, axis=dim)
        leading = lax.slice_in_dim(value, 0, width, axis=dim)
        before = lax.ppermute(last, axis, up)
        after = lax.ppermute(leading, axis, down)
        value = jnp.concatenate([before, value, after], axis=dim)
    return value


def cut_along(value, dim, size):
    before, after = (value.shape[:dim], value.shape[dim + 1 :])
    return jnp.moveaxis(value.reshape(*before, size, -1, *after), dim, 0)


def cut_rows(length, count):
    lap = length // count
    if lap >= 8:
        lap -= lap % 8
    return [lap * k for k in range(1, count)]


def in_order(parts, dim):
    parts = jnp.moveaxis(parts, 0, dim)
    lengths = parts.shape
    return parts.reshape(*lengths[:dim], lengths[dim] * lengths[dim + 1], *lengths[dim + 2 :])


def exchange_in_pieces(value, axis, pieces, split_dim, concat_dim):
    parts = cut_along(value, split_dim, lax.axis_size(axis))
    widest = max(range(1, max(2, parts.ndim - 1)), key=lambda d: parts.shape[d])
    finished = []
    for share in jnp.split(parts, cut_rows(parts.shape[widest], pieces), axis=widest):
        if share.size:
            finished.append(lax.all_to_all(share, axis, split_axis=0, concat_axis=0, tiled=True))
    return in_order(jnp.concatenate(finished, axis=widest), concat_dim)


def advance(upad, kpad):
    lead = (slice(None),) * (upad.ndim - 3)
    middle = (slice(1, -1), slice(1, -1), slice(1, -1))
    near = [
        (slice(2, None), slice(1, -1), slice(1, -1)),
        (slice(0, -2), slice(1, -1), slice(1, -1)),
        (slice(1, -1), slice(2, None), slice(1, -1)),
        (slice(1, -1), slice(0, -2), slice(1, -1)),
        (slice(1, -1), slice(1, -1), slice(2, None)),
        (slice(1, -1), slice(1, -1), slice(0, -2)),
    ]
    field = upad[lead + middle]
    conduct = kpad[lead + middle]
    flux = jnp.zeros_like(field)
    for place in near:
        other = upad[lead + place]
        other_k = kpad[lead + place]
        flux = flux + 0.5 * (conduct + other_k) * (other - field)
    return field + time_step * flux


def run_values(param_levels, param_index):
    levels = jnp.arange(param_levels.shape[1], dtype=jnp.int32)
    picks = (param_index[:, :, None] == levels[None, None, :]).astype(jnp.float32)
    return jnp.sum(picks * param_levels[None, :, :], axis=-1)


def make_features(values):
    count = values.shape[0]
    times = (jnp.arange(STEPS, dtype=jnp.float32) + 1.0) / STEPS
    left = jnp.broadcast_to(values[None], (STEPS, count, values.shape[1]))
    middle = jnp.broadcast_to(times[:, None, None], (STEPS, count, 1))
    right = jnp.ones((STEPS, count, 1), jnp.float32)
    return jnp.concatenate([left, middle, right], axis=-1).reshape(
        STEPS * count, values.shape[1] + 2
    )


def local(base_field, material_map, param_levels, param_index, w_input, w_output):
    values = run_values(param_levels, param_index)
    total_runs = values.shape[0]
    local_runs = total_runs // lax.axis_size("run")
    mine = lax.dynamic_slice_in_dim(values, lax.axis_index("run") * local_runs, local_runs, 0)
    expand = (slice(None), None, None, None)
    cond = jnp.zeros((local_runs,) + material_map.shape, jnp.float32) + mine[:, 0][expand]
    for mat in range(1, 4):
        cond = jnp.where(material_map[None] == mat, mine[:, mat][expand], cond)
    gamma = 0.1 * mine[:, 4][expand]
    field = mine[:, 5][expand] * base_field[None]
    rows_x = base_field.shape[0]
    plane = base_field.shape[1] * base_field.shape[2]
    shots = []
    for step in range(STEPS):
        conduct = cond * (1.0 + gamma * field * field)
        both = jnp.stack([field, conduct])
        padded = padded_2(both.astype(jnp.bfloat16), (("strip", 2),), 1).astype(both.dtype)
        padded = jnp.pad(padded, ((0, 0), (0, 0), (0, 0), (1, 1), (1, 1)))
        field = advance(padded[0], padded[1])
        shot = field.astype(jnp.bfloat16).reshape(local_runs, rows_x, plane)
        shots.append(shot)
    target = exchange_in_pieces(jnp.stack(shots), "run", 2, 3, 1)
    batch = STEPS * total_runs
    goal = target.reshape(batch, -1)
    hid_units = w_output.shape[0]
    weight = w_output.reshape(hid_units, -1)
    features = make_features(values)
    hidden = jnp.tanh(jnp.dot(features, w_input, precision=lax.Precision.HIGHEST))
    hidden_b = hidden.astype(jnp.bfloat16)
    scale = batch ** (-0.5)
    pred = jnp.dot(hidden_b, weight, preferred_element_type=jnp.float32)
    error = ((pred - goal.astype(jnp.float32)) * scale).astype(jnp.bfloat16)
    grad = lax.dot_general(
        hidden_b, error, (((0,), (0,)), ((), ())), preferred_element_type=jnp.float32
    )
    grad_output = grad.astype(jnp.bfloat16).reshape(w_output.shape)
    back = lax.dot_general(
        error, weight, (((1,), (1,)), ((), ())), preferred_element_type=jnp.float32
    )
    slope = back * (1.0 - hidden * hidden)
    partial_grad = jnp.dot(features.T, slope, precision=lax.Precision.HIGHEST)
    grad_input = lax.psum_scatter(partial_grad, ("run", "strip"), scatter_dimension=1, tiled=True)
    return (grad_output, grad_input)


def solution(mesh):
    placed = (
        P("strip", None, None),
        P("strip", None, None),
        P(),
        P(),
        P(),
        P(None, "strip", "run"),
    )
    return jax.shard_map(
        local,
        mesh=mesh,
        in_specs=placed,
        out_specs=(P(None, "strip", "run"), P(None, ("run", "strip"))),
        check_vma=False,
    )
```

profile of v0, /device:TPU:1, one launch (start us, length us, event | category | flops | bytes accessed | tf_op | source)
XLA Modules:
  0.0 462.5 jit_solution(17389501461033258059)
XLA Ops:
  0.6 0.0 copy-start
  0.7 0.8 select_reduce_fusion
  1.4 0.1 constant_dynamic-slice_fusion.1
  1.5 1.2 broadcast_compare_fusion.2
  2.8 1.9 multiply_convert_fusion
  4.7 3.9 collective-permute-start
  8.6 1.3 collective-permute-start.1
  9.9 0.0 collective-permute-done
  9.9 3.3 collective-permute-done.1
  13.3 11.6 %fusion.13 = f32[2,4,66,10,258]{4,3,2,1,0:T(8,128)} fusion(bf16[2,4,1,8,256]{4,3,2,1,0:T(8,128)(2,1)S(1)} %collective-permute-done.1, bf16[2,4,1,8,256]{4,3,2,1,0:T(8,128)(2,1)S(1)} %collective-permute-done, bf16[1,4,64,8,256]{4,3,2,1,0:T(8,128)(2,1)S(1)} %get-tuple-element.27, bf16[1,4,64,8,256]{4,3,2,1,0:T(8,128)(2,1)S(1)} %get-tuple-element.26), kind=kLoop, calls=%fused_computation.38 | loop fusion | flops 31331520 | bytes 7611648 | tf_op jit(solution)/shard_map/jit(_pad)/pad | solution.py:109
  24.9 10.3 %slice_bitcast_fusion.6 = (f32[4,66,10,258]{3,2,1,0:T(8,128)}, f32[4,66,10,258]{3,2,1,0:T(8,128)}) fusion(f32[2,4,66,10,258]{4,3,2,1,0:T(8,128)} %fusion.13), kind=kLoop, calls=%fused_computation.35 | loop fusion | bytes 10897920 | tf_op jit(solution)/shard_map/squeeze | solution.py:110
  35.2 32.9 %fusion.121 = (bf16[4,64,8,256]{3,2,1,0:T(8,128)(2,1)S(1)}, f32[4,64,8,256]{3,2,1,0:T(8,128)S(1)}) fusion(f32[4,66,10,258]{3,2,1,0:T(8,128)} %get-tuple-element.15, f32[4,66,10,258]{3,2,1,0:T(8,128)} %get-tuple-element.14), kind=kLoop, calls=%fused_computation.223 | loop fusion | flops 16777216 | bytes 32505856 | tf_op jit(solution)/shard_map/convert_element_type | solution.py:111
  68.2 0.7 fusion.114
  68.9 3.1 collective-permute-start.2
  72.0 1.3 collective-permute-start.3
  73.3 0.0 collective-permute-done.2
  73.3 3.3 collective-permute-done.3
  76.7 11.6 %fusion.12 = f32[2,4,66,10,258]{4,3,2,1,0:T(8,128)} fusion(bf16[2,4,1,8,256]{4,3,2,1,0:T(8,128)(2,1)S(1)} %collective-permute-done.3, bf16[2,4,1,8,256]{4,3,2,1,0:T(8,128)(2,1)S(1)} %collective-permute-done.2, bf16[1,4,64,8,256]{4,3,2,1,0:T(8,128)(2,1)S(1)} %fusion.114, bf16[1,4,64,8,256]{4,3,2,1,0:T(8,128)(2,1)S(1)} %bitcast.75), kind=kLoop, calls=%fused_computation.32 | loop fusion | flops 31331520 | bytes 7611648 | tf_op jit(solution)/shard_map/jit(_pad)/pad | solution.py:109
  88.3 10.3 %slice_bitcast_fusion.4 = (f32[4,66,10,258]{3,2,1,0:T(8,128)}, f32[4,66,10,258]{3,2,1,0:T(8,128)}) fusion(f32[2,4,66,10,258]{4,3,2,1,0:T(8,128)} %fusion.12), kind=kLoop, calls=%fused_computation.29 | loop fusion | bytes 10897920 | tf_op jit(solution)/shard_map/squeeze | solution.py:110
  98.7 32.9 %fusion.119 = (bf16[4,64,8,256]{3,2,1,0:T(8,128)(2,1)S(1)}, f32[4,64,8,256]{3,2,1,0:T(8,128)S(1)}) fusion(f32[4,66,10,258]{3,2,1,0:T(8,128)} %get-tuple-element.13, f32[4,66,10,258]{3,2,1,0:T(8,128)} %get-tuple-element.12), kind=kLoop, calls=%fused_computation.222 | loop fusion | flops 16777216 | bytes 32505856 | tf_op jit(solution)/shard_map/convert_element_type | solution.py:111
  131.6 0.7 fusion.113
  132.3 4.7 %collective-permute-start.4 = (bf16[2,4,1,8,256]{4,3,2,1,0:T(8,128)(2,1)S(1)}, bf16[2,4,1,8,256]{4,3,2,1,0:T(8,128)(2,1)S(1)}, u32[]{:S(2)}, u32[]{:S(2)}) collective-permute-start(bf16[2,4,1,8,256]{4,3,2,1,0:T(8,128)(2,1)S(1)} %get-tuple-element.20), channel_id=1, source_target_pairs={{0,1},{1,2},{2,3},{3,4},{4,5},{5,6},{6,7},{8,9},{9,10},{10,11},{11... | collective-permute-start | bytes 98312 | tf_op jit(solution)/shard_map/ppermute | solution.py:19
  137.0 1.6 collective-permute-start.5
  138.7 0.0 collective-permute-done.4
  138.7 3.4 collective-permute-done.5
  142.0 11.6 %fusion.11 = f32[2,4,66,10,258]{4,3,2,1,0:T(8,128)} fusion(bf16[2,4,1,8,256]{4,3,2,1,0:T(8,128)(2,1)S(1)} %collective-permute-done.5, bf16[2,4,1,8,256]{4,3,2,1,0:T(8,128)(2,1)S(1)} %collective-permute-done.4, bf16[1,4,64,8,256]{4,3,2,1,0:T(8,128)(2,1)S(1)} %fusion.113, bf16[1,4,64,8,256]{4,3,2,1,0:T(8,128)(2,1)S(1)} %bitcast.77), kind=kLoop, calls=%fused_computation.26 | loop fusion | flops 31331520 | bytes 7611648 | tf_op jit(solution)/shard_map/jit(_pad)/pad | solution.py:109
  153.7 10.3 %slice_bitcast_fusion.2 = (f32[4,66,10,258]{3,2,1,0:T(8,128)}, f32[4,66,10,258]{3,2,1,0:T(8,128)}) fusion(f32[2,4,66,10,258]{4,3,2,1,0:T(8,128)} %fusion.11), kind=kLoop, calls=%fused_computation.23 | loop fusion | bytes 10897920 | tf_op jit(solution)/shard_map/squeeze | solution.py:110
  164.0 32.9 %fusion.117 = (bf16[4,64,8,256]{3,2,1,0:T(8,128)(2,1)S(1)}, f32[4,64,8,256]{3,2,1,0:T(8,128)S(1)}) fusion(f32[4,66,10,258]{3,2,1,0:T(8,128)} %get-tuple-element.11, f32[4,66,10,258]{3,2,1,0:T(8,128)} %get-tuple-element.10), kind=kLoop, calls=%fused_computation.221 | loop fusion | flops 16777216 | bytes 32505856 | tf_op jit(solution)/shard_map/convert_element_type | solution.py:111
  197.0 0.7 fusion.112
  197.7 0.0 copy-start.1
  197.7 1.0 copy-done.1
  198.7 4.0 collective-permute-start.6
  202.7 1.3 collective-permute-start.7
  204.0 1.2 stack.54
  205.2 1.2 stack.58
  206.4 1.2 stack.62
  207.6 0.0 collective-permute-done.6
  207.6 0.0 collective-permute-done.7
  207.6 11.7 %fusion.10 = f32[2,4,66,10,258]{4,3,2,1,0:T(8,128)} fusion(bf16[2,4,1,8,256]{4,3,2,1,0:T(8,128)(2,1)S(1)} %collective-permute-done.7, bf16[2,4,1,8,256]{4,3,2,1,0:T(8,128)(2,1)S(1)} %collective-permute-done.6, bf16[1,4,64,8,256]{4,3,2,1,0:T(8,128)(2,1)S(1)} %copy-done.2, bf16[1,4,64,8,256]{4,3,2,1,0:T(8,128)(2,1)S(1)} %bitcast.79), kind=kLoop, calls=%fused_computation.20 | loop fusion | flops 31331520 | bytes 7611648 | tf_op jit(solution)/shard_map/jit(_pad)/pad | solution.py:109
  219.2 10.3 %slice_bitcast_fusion = (f32[4,66,10,258]{3,2,1,0:T(8,128)}, f32[4,66,10,258]{3,2,1,0:T(8,128)}) fusion(f32[2,4,66,10,258]{4,3,2,1,0:T(8,128)} %fusion.10), kind=kLoop, calls=%fused_computation.17 | loop fusion | bytes 10897920 | tf_op jit(solution)/shard_map/squeeze | solution.py:110
  229.6 33.7 %fusion.36 = bf16[4,64,8,256]{3,2,1,0:T(8,128)(2,1)} fusion(f32[4,66,10,258]{3,2,1,0:T(8,128)} %get-tuple-element.9, f32[4,66,10,258]{3,2,1,0:T(8,128)} %get-tuple-element.8), kind=kLoop, calls=%fused_computation.70 | loop fusion | flops 16777216 | bytes 30408704 | tf_op jit(solution)/shard_map/convert_element_type | solution.py:111
  263.3 2.3 stack.66
  265.7 1.6 maximum_bitcast_fusion
  267.3 2.2 fusion.123
  269.5 1.8 copy.23
  271.4 13.3 %all-to-all-start = ((bf16[16,4,4,32,128]{4,3,2,1,0:T(8,128)(2,1)}), bf16[16,4,4,32,128]{4,3,2,1,0:T(8,128)(2,1)S(1)}, u32[]{:S(2)}, u32[]{:S(2)}) async-start(bf16[16,4,4,32,128]{4,3,2,1,0:T(8,128)(2,1)} %copy.23), calls=%async_computation | async-start | bytes 4194304 | tf_op jit(solution)/shard_map/all_to_all | solution.py:49
  284.6 3.5 copy.24
  288.1 24.9 %all-to-all-done = bf16[16,4,4,32,128]{4,3,2,1,0:T(8,128)(2,1)S(1)} async-done(((bf16[16,4,4,32,128]{4,3,2,1,0:T(8,128)(2,1)}), bf16[16,4,4,32,128]{4,3,2,1,0:T(8,128)(2,1)S(1)}, u32[]{:S(2)}, u32[]{:S(2)}) %all-to-all-start) | async-done | bytes 2097184 | tf_op jit(solution)/shard_map/all_to_all | solution.py:49
  313.0 5.3 %all-to-all-start.1 = ((bf16[16,4,4,32,128]{4,3,2,1,0:T(8,128)(2,1)}), bf16[16,4,4,32,128]{4,3,2,1,0:T(8,128)(2,1)}, u32[]{:S(2)}, u32[]{:S(2)}) async-start(bf16[16,4,4,32,128]{4,3,2,1,0:T(8,128)(2,1)} %copy.24), calls=%async_computation.1 | async-start | bytes 4194304 | tf_op jit(solution)/shard_map/all_to_all | solution.py:49
  318.3 0.1 pad.65.clone
  318.4 0.1 broadcast_in_dim.77
  318.5 0.1 maximum_maximum_fusion
  318.6 0.1 reshape.79
  318.6 0.6 convolution_tanh_fusion
  319.3 27.4 %all-to-all-done.1 = bf16[16,4,4,32,128]{4,3,2,1,0:T(8,128)(2,1)} async-done(((bf16[16,4,4,32,128]{4,3,2,1,0:T(8,128)(2,1)}), bf16[16,4,4,32,128]{4,3,2,1,0:T(8,128)(2,1)}, u32[]{:S(2)}, u32[]{:S(2)}) %all-to-all-start.1) | async-done | bytes 2097184 | tf_op jit(solution)/shard_map/all_to_all | solution.py:49
  346.7 2.7 convert_bitcast_fusion
  349.4 1.7 copy.25
  351.0 13.8 %fusion.4 = bf16[256,8192]{1,0:T(8,128)(2,1)S(1)} fusion(f32[32,8,64,128]{3,2,1,0:T(8,128)S(1)} %bitcast.73, bf16[64,8,64,128]{3,2,1,0:T(8,128)(2,1)} %bitcast.81, f32[256,512]{1,0:T(8,128)S(1)} %convolution_tanh_fusion), kind=kOutput, calls=%fused_computation.10 | convolution fusion | flops 2153906176 | bytes 21495808 | tf_op jit(solution)/shard_map/dot_general | solution.py:122
  364.9 5.7 %fusion.19 = bf16[64,8,64,128]{3,1,2,0:T(8,128)(2,1)} fusion(bf16[256,8192]{1,0:T(8,128)(2,1)S(1)} %fusion.4, f32[256,512]{1,0:T(8,128)S(1)} %convolution_tanh_fusion), kind=kOutput, calls=%fused_computation.45 | convolution fusion | flops 2151809024 | bytes 13107200 | tf_op jit(solution)/shard_map/dot_general | solution.py:124
  370.5 12.3 %fusion.109 = f32[256,512]{1,0:T(8,128)S(1)} fusion(bf16[256,8192]{1,0:T(8,128)(2,1)S(1)} %fusion.4, bf16[64,8,64,128]{3,2,1,0:T(8,128)(2,1)} %bitcast.82, f32[256,512]{1,0:T(8,128)S(1)} %convolution_tanh_fusion), kind=kOutput, calls=%fused_computation.192 | convolution fusion | flops 2147876864 | bytes 13631488 | tf_op jit(solution)/shard_map/dot_general | solution.py:128
  382.9 9.7 %copy.28 = bf16[64,8,64,128]{3,2,1,0:T(8,128)(2,1)} copy(bf16[64,8,64,128]{3,1,2,0:T(8,128)(2,1)} %fusion.19) | data formatting | bytes 16777216
  392.6 1.0 fusion.124
  393.6 67.9 %all-reduce.4 = f32[8,512]{0,1:T(8,128)S(1)} all-reduce(f32[8,512]{0,1:T(8,128)S(1)} %fusion.124), channel_id=2, replica_groups=mesh['run'=16,'strip'=8] {'run','strip'}, use_global_device_ids=true, to_apply=%region_1.2.clone | all-reduce | flops 4096 | bytes 32768
  461.5 0.6 constant_dynamic-slice_fusion
  (17 shorter events, 0.1 us)
Async XLA Ops:
  0.6 318.0 %copy-start = (f32[8,512]{1,0:T(8,128)S(1)}, f32[8,512]{1,0:T(8,128)}, u32[]{:S(2)}) copy-start(f32[8,512]{1,0:T(8,128)} %param.10) | copy-start | bytes 49156
  4.7 5.2 %collective-permute-start = (bf16[2,4,1,8,256]{4,3,2,1,0:T(8,128)(2,1)S(1)}, bf16[2,4,1,8,256]{4,3,2,1,0:T(8,128)(2,1)S(1)}, u32[]{:S(2)}, u32[]{:S(2)}) collective-permute-start(bf16[2,4,1,8,256]{4,3,2,1,0:T(8,128)(2,1)S(1)} %get-tuple-element.24), channel_id=1, source_target_pairs={{0,1},{1,2},{2,3},{3,4},{4,5},{5,6},{6,7},{8,9},{9,10},{10,11},{11... | collective-permute-start | bytes 98312 | tf_op jit(solution)/shard_map/ppermute | solution.py:19
  8.6 4.7 %collective-permute-start.1 = (bf16[2,4,1,8,256]{4,3,2,1,0:T(8,128)(2,1)S(1)}, bf16[2,4,1,8,256]{4,3,2,1,0:T(8,128)(2,1)S(1)}, u32[]{:S(2)}, u32[]{:S(2)}) collective-permute-start(bf16[2,4,1,8,256]{4,3,2,1,0:T(8,128)(2,1)S(1)} %get-tuple-element.25), channel_id=1, source_target_pairs={{1,0},{2,1},{3,2},{4,3},{5,4},{6,5},{7,6},{9,8},{10,9},{11,10},{12... | collective-permute-start | bytes 98312 | tf_op jit(solution)/shard_map/ppermute | solution.py:20
  68.9 4.4 collective-permute-start.2
  72.0 4.7 %collective-permute-start.3 = (bf16[2,4,1,8,256]{4,3,2,1,0:T(8,128)(2,1)S(1)}, bf16[2,4,1,8,256]{4,3,2,1,0:T(8,128)(2,1)S(1)}, u32[]{:S(2)}, u32[]{:S(2)}) collective-permute-start(bf16[2,4,1,8,256]{4,3,2,1,0:T(8,128)(2,1)S(1)} %get-tuple-element.23), channel_id=1, source_target_pairs={{1,0},{2,1},{3,2},{4,3},{5,4},{6,5},{7,6},{9,8},{10,9},{11,10},{12... | collective-permute-start | bytes 98312 | tf_op jit(solution)/shard_map/ppermute | solution.py:20
  132.3 6.3 %collective-permute-start.4 = (bf16[2,4,1,8,256]{4,3,2,1,0:T(8,128)(2,1)S(1)}, bf16[2,4,1,8,256]{4,3,2,1,0:T(8,128)(2,1)S(1)}, u32[]{:S(2)}, u32[]{:S(2)}) collective-permute-start(bf16[2,4,1,8,256]{4,3,2,1,0:T(8,128)(2,1)S(1)} %get-tuple-element.20), channel_id=1, source_target_pairs={{0,1},{1,2},{2,3},{3,4},{4,5},{5,6},{6,7},{8,9},{9,10},{10,11},{11... | collective-permute-start | bytes 98312 | tf_op jit(solution)/shard_map/ppermute | solution.py:19
  137.0 5.0 %collective-permute-start.5 = (bf16[2,4,1,8,256]{4,3,2,1,0:T(8,128)(2,1)S(1)}, bf16[2,4,1,8,256]{4,3,2,1,0:T(8,128)(2,1)S(1)}, u32[]{:S(2)}, u32[]{:S(2)}) collective-permute-start(bf16[2,4,1,8,256]{4,3,2,1,0:T(8,128)(2,1)S(1)} %get-tuple-element.21), channel_id=1, source_target_pairs={{1,0},{2,1},{3,2},{4,3},{5,4},{6,5},{7,6},{9,8},{10,9},{11,10},{12... | collective-permute-start | bytes 98312 | tf_op jit(solution)/shard_map/ppermute | solution.py:20
  197.7 1.0 copy-start.1
  198.7 8.9 %collective-permute-start.6 = (bf16[2,4,1,8,256]{4,3,2,1,0:T(8,128)(2,1)S(1)}, bf16[2,4,1,8,256]{4,3,2,1,0:T(8,128)(2,1)S(1)}, u32[]{:S(2)}, u32[]{:S(2)}) collective-permute-start(bf16[2,4,1,8,256]{4,3,2,1,0:T(8,128)(2,1)S(1)} %get-tuple-element.18), channel_id=1, source_target_pairs={{0,1},{1,2},{2,3},{3,4},{4,5},{5,6},{6,7},{8,9},{9,10},{10,11},{11... | collective-permute-start | bytes 98312 | tf_op jit(solution)/shard_map/ppermute | solution.py:19
  202.7 4.9 %collective-permute-start.7 = (bf16[2,4,1,8,256]{4,3,2,1,0:T(8,128)(2,1)S(1)}, bf16[2,4,1,8,256]{4,3,2,1,0:T(8,128)(2,1)S(1)}, u32[]{:S(2)}, u32[]{:S(2)}) collective-permute-start(bf16[2,4,1,8,256]{4,3,2,1,0:T(8,128)(2,1)S(1)} %get-tuple-element.19), channel_id=1, source_target_pairs={{1,0},{2,1},{3,2},{4,3},{5,4},{6,5},{7,6},{9,8},{10,9},{11,10},{12... | collective-permute-start | bytes 98312 | tf_op jit(solution)/shard_map/ppermute | solution.py:20
  205.2 2.4 copy-start.2
  229.6 36.1 %copy-start.5 = (bf16[1,4,64,16,128]{4,3,2,1,0:T(8,128)(2,1)S(1)}, bf16[1,4,64,16,128]{4,3,2,1,0:T(8,128)(2,1)}, u32[]{:S(2)}) copy-start(bf16[1,4,64,16,128]{4,3,2,1,0:T(8,128)(2,1)} %stack.62) | copy-start | bytes 3145732
  263.3 2.4 copy-start.3
  263.3 2.4 copy-start.4
  271.4 41.6 %all-to-all-start = ((bf16[16,4,4,32,128]{4,3,2,1,0:T(8,128)(2,1)}), bf16[16,4,4,32,128]{4,3,2,1,0:T(8,128)(2,1)S(1)}, u32[]{:S(2)}, u32[]{:S(2)}) async-start(bf16[16,4,4,32,128]{4,3,2,1,0:T(8,128)(2,1)} %copy.23), calls=%async_computation | async-start | bytes 4194304 | tf_op jit(solution)/shard_map/all_to_all | solution.py:49
  313.0 33.7 %all-to-all-start.1 = ((bf16[16,4,4,32,128]{4,3,2,1,0:T(8,128)(2,1)}), bf16[16,4,4,32,128]{4,3,2,1,0:T(8,128)(2,1)}, u32[]{:S(2)}, u32[]{:S(2)}) async-start(bf16[16,4,4,32,128]{4,3,2,1,0:T(8,128)(2,1)} %copy.24), calls=%async_computation.1 | async-start | bytes 4194304 | tf_op jit(solution)/shard_map/all_to_all | solution.py:49
where the time goes:
time: 472 us; the launch traced here: 463 us
  other arithmetic  189 us (40%)
  local copies, waits for them, and re-layouts  68.1 us (14%)
  blocking collectives  67.9 us (14%)
  waiting for transfers between devices  62.4 us (13%)
  starting transfers between devices  39.9 us (8%)
  matrix products  33.5 us (7%)
    convert_element_type x4, other arithmetic, local(): shot = field.astype(jnp.bfloat16).reshape(local_runs, rows_x, plane)  133 us
    unnamed x1, blocking collectives  67.9 us
    all_to_all x2, waiting for transfers between devices, exchange_in_pieces(): lax.all_to_all(share, axis, split_axis=0, concat_axis=0, tiled=True)  52.3 us
    pad x4, other arithmetic, local(): padded = jnp.pad(padded, ((0, 0), (0, 0), (0, 0), (1, 1), (1, 1)))  46.5 us
    squeeze x4, local copies, waits for them, and re-layouts, local(): field = advance(padded[0], padded[1])  41.4 us
    all_to_all x2, starting transfers between devices, exchange_in_pieces(): lax.all_to_all(share, axis, split_axis=0, concat_axis=0, tiled=True)  18.6 us
    ppermute x4, starting transfers between devices, padded_2(): before = lax.ppermute(last, axis, up)  15.8 us
    dot_general x1, matrix products, local(): pred = jnp.dot(hidden_b, weight, preferred_element_type=jnp.float32)  13.8 us
  transfers between devices with their start and end apart: 10, of which 5 were waited for; matrix products, arithmetic and copies ran while one was open for 2% of the time, Pallas kernels for 0%

commit v1 on v0

v1 whole, which is shorter than its diff:
```python
import functools

import jax
import jax.numpy as jnp
from jax import lax
from jax.experimental import pallas as pl
from jax.experimental.pallas import tpu as pltpu
from jax.sharding import PartitionSpec as P

STEPS = 4
TIME_STEP = 0.08
BF = jnp.bfloat16
F32 = jnp.float32
MESH = pl.DeviceIdType.MESH
GROUP = 16
LANES = 128


def run_column(levels_ref, index, p):
    col = index[:, p : p + 1]
    out = jnp.zeros(col.shape, F32)
    for level in range(levels_ref.shape[1]):
        out = jnp.where(col == level, levels_ref[p, level], out)
    return out


def stencil_kernel(
    n_strip, levels, index, base, material, out,
    bx, mx, u_a, u_b, k_a, k_b, cond, cond_g, shots,
    local_sem, halo_send, halo_recv, keep_sem, send_sem, recv_sem,
):
    rows_x, nz, ny = base.shape
    ext = rows_x + 2 * STEPS
    run = lax.axis_index("run")
    strip = lax.axis_index("strip")
    core = lax.rem(run, 2)
    slab = lax.div(run, 2)
    partner = run + 1 - 2 * core
    right = lax.rem(strip + 1, n_strip)
    left = lax.rem(strip + n_strip - 1, n_strip)

    local = [
        pltpu.make_async_copy(src, dst.at[pl.ds(STEPS, rows_x)], local_sem.at[i])
        for i, (src, dst) in enumerate(((base, bx), (material, mx)))
    ]
    for copy in local:
        copy.start()
    barrier = pltpu.get_barrier_semaphore()
    for where in ({"strip": left}, {"strip": right}, {"run": partner}):
        pl.semaphore_signal(barrier, inc=1, device_id=where, device_id_type=MESH)
    pl.semaphore_wait(barrier, 3)
    halos = []
    for i, (src, dst) in enumerate(((base, bx), (material, mx))):
        for j, (first, to, target) in enumerate(
            ((rows_x - STEPS, 0, right), (0, STEPS + rows_x, left))
        ):
            copy = pltpu.make_async_remote_copy(
                src_ref=src.at[pl.ds(first, STEPS)],
                dst_ref=dst.at[pl.ds(to, STEPS)],
                send_sem=halo_send.at[2 * i + j],
                recv_sem=halo_recv.at[2 * i + j],
                device_id={"strip": target},
                device_id_type=MESH,
            )
            copy.start()
            halos.append(copy)

    zero_row = jnp.zeros((GROUP, ny), BF)

    def clear(pad):
        def body(x, carry):
            for ref in (u_a, u_b, k_a, k_b):
                ref[pad, x] = zero_row
            return carry

        lax.fori_loop(0, ext, body, 0)

    clear(0)
    clear(nz + 1)
    for copy in local:
        copy.wait()

    lane = lax.broadcasted_iota(jnp.int32, (GROUP, LANES), 1).astype(F32).astype(BF)
    first_lane = lane == jnp.asarray(0, BF)
    last_lane = lane == jnp.asarray(LANES - 1, BF)
    zero = jnp.zeros((GROUP, LANES), BF)

    def prepare(g):
        picks = index[pl.ds(pl.multiple_of(core * 2 * GROUP + g * GROUP, GROUP), GROUP), :]
        vals = [run_column(levels, picks, p) for p in range(6)]
        wide = lambda col: jnp.broadcast_to(col, (GROUP, LANES))
        kinds = [wide(0.5 * TIME_STEP * vals[m]).astype(BF) for m in range(4)]
        growth = 0.1 * vals[4]
        kinds_g = [wide(0.5 * TIME_STEP * vals[m] * growth).astype(BF) for m in range(4)]
        start = wide(vals[5])
        return kinds, kinds_g, start

    def fill(first, count, unroll, kinds, kinds_g, start):
        def one(x):
            tile = bx[x]
            mats = mx[x].astype(F32)
            for z in range(nz):
                for h in range(2):
                    cut = slice(h * LANES, (h + 1) * LANES)
                    mat = jnp.broadcast_to(mats[z : z + 1, cut], (GROUP, LANES)).astype(BF)
                    c, cg = kinds[0], kinds_g[0]
                    for m in range(1, 4):
                        hit = mat == jnp.asarray(m, BF)
                        c = jnp.where(hit, kinds[m], c)
                        cg = jnp.where(hit, kinds_g[m], cg)
                    u = (jnp.broadcast_to(tile[z : z + 1, cut], (GROUP, LANES)) * start).astype(BF)
                    cond[z, x, :, cut] = c
                    cond_g[z, x, :, cut] = cg
                    u_a[z + 1, x, :, cut] = u
                    k_a[z + 1, x, :, cut] = c + cg * (u * u)

        def body(i, carry):
            for j in range(unroll):
                one(first + i * unroll + j)
            return carry

        lax.fori_loop(0, count // unroll, body, 0)

    def blank(refs, first, count):
        def body(z, carry):
            for x in range(first, first + count):
                for ref, shift in refs:
                    ref[z + shift, x] = zero_row
            return carry

        lax.fori_loop(0, nz, body, 0)

    def advance(step, g, us, ks, ud, kd):
        rows = ext - 2 * step
        unroll = {70: 14, 68: 17, 66: 22, 64: 16}.get(rows, 1)
        reach = STEPS - step
        final = step == STEPS
        low = jnp.maximum(slab - reach, 0)
        high = jnp.minimum(slab + reach, nz - 1)

        def slab_body(z, carry):
            zp = z + 1

            def halves(ref, a, x):
                row = ref[a, x]
                return [row[:, :LANES], row[:, LANES:]]

            u0, k0 = halves(us, zp, step), halves(ks, zp, step)
            ub, kb = halves(us, zp, step - 1), halves(ks, zp, step - 1)
            fl0 = [(k0[h] + kb[h]) * (u0[h] - ub[h]) for h in range(2)]

            def cell(x, u, k, fl):
                un, kn = halves(us, zp, x + 1), halves(ks, zp, x + 1)
                uu, ku = halves(us, zp + 1, x), halves(ks, zp + 1, x)
                ul, kl = halves(us, zp - 1, x), halves(ks, zp - 1, x)
                ru = [pltpu.roll(v, LANES - 1, 1) for v in u]
                rk = [pltpu.roll(v, LANES - 1, 1) for v in k]
                up = [jnp.where(last_lane, ru[1], ru[0]), jnp.where(last_lane, zero, ru[1])]
                kp = [jnp.where(last_lane, rk[1], rk[0]), jnp.where(last_lane, zero, rk[1])]
                fy = [(k[h] + kp[h]) * (up[h] - u[h]) for h in range(2)]
                rf = [pltpu.roll(v, 1, 1) for v in fy]
                fyl = [jnp.where(first_lane, k[0] * u[0], rf[0]), jnp.where(first_lane, rf[0], rf[1])]
                fr = []
                for h in range(2):
                    face = (k[h] + kn[h]) * (un[h] - u[h])
                    top = (k[h] + ku[h]) * (uu[h] - u[h])
                    low_face = (k[h] + kl[h]) * (u[h] - ul[h])
                    total = (face - fl[h]) + (top - low_face) + (fy[h] - fyl[h])
                    new = u[h] + total
                    cut = slice(h * LANES, (h + 1) * LANES)
                    if final:
                        shots[h, step - 1, g, x - STEPS] = new
                    else:
                        ud[zp, x, :, cut] = new
                        kd[zp, x, :, cut] = cond[z, x, :, cut] + cond_g[z, x, :, cut] * (new * new)
                    fr.append(face)
                return un, kn, fr

            def body(i, carry):
                u, k, fl = carry
                for j in range(unroll):
                    u, k, fl = cell(step + i * unroll + j, u, k, fl)
                return u, k, fl

            lax.fori_loop(0, rows // unroll, body, (u0, k0, fl0))
            return carry

        lax.fori_loop(low, high + 1, slab_body, 0)
        if not final:

            @pl.when(strip == 0)
            def _():
                blank([(ud, 1)], 0, STEPS)

            @pl.when(strip == n_strip - 1)
            def _():
                blank([(ud, 1)], STEPS + rows_x, STEPS)

            def keep(i, carry):
                for j in range(8):
                    x = i * 8 + j
                    for h in range(2):
                        shots[h, step - 1, g, x] = ud[slab + 1, x + STEPS, :, h * LANES : (h + 1) * LANES]
                return carry

            lax.fori_loop(0, rows_x // 8, keep, 0)

    def sends(step, g):
        mine = pltpu.make_async_copy(
            shots.at[core, step - 1, g], out.at[core, step - 1, g], keep_sem.at[step - 1, g]
        )
        away = pltpu.make_async_remote_copy(
            src_ref=shots.at[1 - core, step - 1, g],
            dst_ref=out.at[core, step - 1, g],
            send_sem=send_sem.at[step - 1, g],
            recv_sem=recv_sem.at[step - 1, g],
            device_id={"run": partner},
            device_id_type=MESH,
        )
        return mine, away

    def group(g, carry):
        consts = prepare(g)
        fill(STEPS, rows_x, 2, *consts)

        @pl.when(g == 0)
        def _():
            for copy in halos:
                copy.wait()

        fill(0, STEPS, 2, *consts)
        fill(STEPS + rows_x, STEPS, 2, *consts)
        everywhere = [(cond, 0), (cond_g, 0), (u_a, 1), (k_a, 1)]

        @pl.when(strip == 0)
        def _():
            blank(everywhere, 0, STEPS)

        @pl.when(strip == n_strip - 1)
        def _():
            blank(everywhere, STEPS + rows_x, STEPS)

        pairs = [(u_a, k_a), (u_b, k_b)]
        for step in range(1, STEPS + 1):
            src, dst = pairs[(step - 1) % 2], pairs[step % 2]
            advance(step, g, *src, *dst)
            for copy in sends(step, g):
                copy.start()
        return carry

    lax.fori_loop(0, 2, group, 0)
    for g in range(2):
        for step in range(1, STEPS + 1):
            for copy in sends(step, g):
                copy.wait()


def snapshots(levels, index, base, material, n_strip):
    rows_x, nz, ny = base.shape
    ext = rows_x + 2 * STEPS
    hbm = pl.BlockSpec(memory_space=pl.ANY)
    field = pltpu.VMEM((nz + 2, ext, GROUP, ny), BF)
    inner = pltpu.VMEM((nz, ext, GROUP, ny), BF)
    return pl.pallas_call(
        functools.partial(stencil_kernel, n_strip),
        out_shape=jax.ShapeDtypeStruct((2, STEPS, 2, rows_x, GROUP, LANES), BF),
        in_specs=[
            pl.BlockSpec(memory_space=pltpu.SMEM),
            pl.BlockSpec(memory_space=pltpu.VMEM),
            hbm,
            hbm,
        ],
        out_specs=hbm,
        scratch_shapes=[
            pltpu.VMEM((ext, nz, ny), F32),
            pltpu.VMEM((ext, nz, ny), jnp.int32),
            field, field, field, field, inner, inner,
            pltpu.VMEM((2, STEPS, 2, rows_x, GROUP, LANES), BF),
            pltpu.SemaphoreType.DMA((2,)),
            pltpu.SemaphoreType.DMA((4,)),
            pltpu.SemaphoreType.DMA((4,)),
            pltpu.SemaphoreType.DMA((STEPS, 2)),
            pltpu.SemaphoreType.DMA((STEPS, 2)),
            pltpu.SemaphoreType.DMA((STEPS, 2)),
        ],
        compiler_params=pltpu.CompilerParams(
            collective_id=0, has_side_effects=True, vmem_limit_bytes=63 * 1024 * 1024
        ),
        name="snapshots",
    )(levels, index, base, material)


def training_kernel(levels, index, w_in, weight, target, grad, partial, hid, hid_b, hid_t, back):
    step = pl.program_id(0)
    half = 2 * GROUP
    units, width, _ = weight.shape
    batch = hid.shape[0]

    @pl.when(step == 0)
    def _():
        picks = index[...]
        total = jnp.zeros((picks.shape[0], units), F32)
        for p in range(6):
            total = total + run_column(levels, picks, p) * w_in[p : p + 1, :]
        for core in range(2):
            for t in range(STEPS):
                rows = total[core * half : (core + 1) * half]
                pre = rows + ((t + 1.0) / STEPS) * w_in[6:7, :] + w_in[7:8, :]
                hid[pl.ds((core * STEPS + t) * half, half), :] = jnp.tanh(pre)
        hid_b[...] = hid[...].astype(BF)
        hid_t[...] = hid[...].T.astype(BF)
        back[...] = jnp.zeros_like(back)

    w = jnp.swapaxes(weight[...], 0, 1)
    w = jnp.concatenate([w[x] for x in range(width)], axis=1)
    pred = jnp.dot(hid_b[...], w, preferred_element_type=F32)
    goal = jnp.concatenate(
        [target[:, :, :, x].reshape(batch, LANES) for x in range(width)], axis=1
    )
    error = ((pred - goal.astype(F32)) * (batch ** -0.5)).astype(BF)
    g = jnp.dot(hid_t[...], error, preferred_element_type=F32).astype(BF)
    g = jnp.stack([g[:, x * LANES : (x + 1) * LANES] for x in range(width)], axis=0)
    grad[...] = jnp.swapaxes(g, 0, 1)
    back[...] += lax.dot_general(error, w, (((1,), (1,)), ((), ())), preferred_element_type=F32)

    @pl.when(step == pl.num_programs(0) - 1)
    def _():
        picks = index[...]
        h = hid[...]
        slope = back[...] * (1.0 - h * h)
        by_step = [
            jnp.concatenate(
                [slope[(core * STEPS + t) * half : (core * STEPS + t + 1) * half] for core in range(2)],
                axis=0,
            )
            for t in range(STEPS)
        ]
        runs = by_step[0] + by_step[1] + by_step[2] + by_step[3]
        rows = [jnp.sum(run_column(levels, picks, p) * runs, axis=0, keepdims=True) for p in range(6)]
        timed = sum(((t + 1.0) / STEPS) * by_step[t] for t in range(STEPS))
        rows.append(jnp.sum(timed, axis=0, keepdims=True))
        rows.append(jnp.sum(runs, axis=0, keepdims=True))
        full = jnp.concatenate(rows, axis=0)
        for q in range(units // LANES):
            partial[q] = full[:, q * LANES : (q + 1) * LANES]


def training(levels, index, w_in, weight, target):
    units, rows_x, _ = weight.shape
    width = 8
    batch = STEPS * index.shape[0]
    vmem = pl.BlockSpec(memory_space=pltpu.VMEM)
    return pl.pallas_call(
        training_kernel,
        grid=(rows_x // width,),
        out_shape=(
            jax.ShapeDtypeStruct(weight.shape, BF),
            jax.ShapeDtypeStruct((units // LANES, 8, LANES), F32),
        ),
        in_specs=[
            pl.BlockSpec(memory_space=pltpu.SMEM),
            vmem,
            vmem,
            pl.BlockSpec((units, width, LANES), lambda i: (0, i, 0)),
            pl.BlockSpec((2, STEPS, 2, width, GROUP, LANES), lambda i: (0, 0, 0, i, 0, 0)),
        ],
        out_specs=(
            pl.BlockSpec((units, width, LANES), lambda i: (0, i, 0)),
            pl.BlockSpec((units // LANES, 8, LANES), lambda i: (0, 0, 0)),
        ),
        scratch_shapes=[
            pltpu.VMEM((batch, units), F32),
            pltpu.VMEM((batch, units), BF),
            pltpu.VMEM((units, batch), BF),
            pltpu.VMEM((batch, units), F32),
        ],
        compiler_params=pltpu.CompilerParams(
            dimension_semantics=("arbitrary",), vmem_limit_bytes=48 * 1024 * 1024
        ),
        name="training",
    )(levels, index, w_in, weight, target)


def reduce_kernel(n_run, n_strip, partial, out, got_run, mid, got_strip, s_run, r_run, s_strip, r_strip):
    run = lax.axis_index("run")
    strip = lax.axis_index("strip")
    per = LANES // (partial.shape[0] * LANES // n_run)
    barrier = pltpu.get_barrier_semaphore()
    peers = [{"run": lax.rem(run + j, n_run)} for j in range(1, n_run)]
    peers += [{"strip": lax.rem(strip + j, n_strip)} for j in range(1, n_strip)]
    for where in peers:
        pl.semaphore_signal(barrier, inc=1, device_id=where, device_id_type=MESH)
    pl.semaphore_wait(barrier, n_run + n_strip - 2)
    copies = []
    for j in range(1, n_run):
        to = lax.rem(run + j, n_run)
        copies.append(
            pltpu.make_async_remote_copy(
                src_ref=partial.at[lax.div(to, per)],
                dst_ref=got_run.at[j - 1],
                send_sem=s_run.at[j - 1],
                recv_sem=r_run.at[j - 1],
                device_id={"run": to},
                device_id_type=MESH,
            )
        )
        copies[-1].start()
    total = partial[lax.div(run, per)]
    for j in range(n_run - 1):
        copies[j].wait_recv()
        total = total + got_run[j]
    mid[...] = total
    more = []
    for j in range(1, n_strip):
        to = lax.rem(strip + j, n_strip)
        more.append(
            pltpu.make_async_remote_copy(
                src_ref=mid,
                dst_ref=got_strip.at[j - 1],
                send_sem=s_strip.at[j - 1],
                recv_sem=r_strip.at[j - 1],
                device_id={"strip": to},
                device_id_type=MESH,
            )
        )
        more[-1].start()
    for j in range(n_strip - 1):
        more[j].wait_recv()
        total = total + got_strip[j]
    for copy in copies + more:
        copy.wait_send()
    keep = out.shape[1]
    at = lax.rem(run, per) * (n_strip * keep) + strip * keep
    out[...] = pltpu.roll(total, lax.rem(LANES - at, LANES), 1)[:, :keep]


def reduced(partial, n_run, n_strip):
    units = partial.shape[0] * LANES
    vmem = pl.BlockSpec(memory_space=pltpu.VMEM)
    return pl.pallas_call(
        functools.partial(reduce_kernel, n_run, n_strip),
        out_shape=jax.ShapeDtypeStruct((8, units // (n_run * n_strip)), F32),
        in_specs=[vmem],
        out_specs=vmem,
        scratch_shapes=[
            pltpu.VMEM((n_run - 1, 8, LANES), F32),
            pltpu.VMEM((8, LANES), F32),
            pltpu.VMEM((n_strip - 1, 8, LANES), F32),
            pltpu.SemaphoreType.DMA((n_run - 1,)),
            pltpu.SemaphoreType.DMA((n_run - 1,)),
            pltpu.SemaphoreType.DMA((n_strip - 1,)),
            pltpu.SemaphoreType.DMA((n_strip - 1,)),
        ],
        compiler_params=pltpu.CompilerParams(collective_id=1, has_side_effects=True),
        name="reduced",
    )(partial)


def solution(mesh):
    n_run, n_strip = mesh.shape["run"], mesh.shape["strip"]

    def local(base_field, material_map, param_levels, param_index, w_input, w_output):
        target = snapshots(param_levels, param_index, base_field, material_map, n_strip)
        grad_output, partial = training(param_levels, param_index, w_input, w_output, target)
        return grad_output, reduced(partial, n_run, n_strip)

    placed = (
        P("strip", None, None),
        P("strip", None, None),
        P(),
        P(),
        P(),
        P(None, "strip", "run"),
    )
    return jax.shard_map(
        local,
        mesh=mesh,
        in_specs=placed,
        out_specs=(P(None, "strip", "run"), P(None, ("run", "strip"))),
        check_vma=False,
    )
```

time: 472 us -> 97.5 us (0.21); the launches traced: 463 us -> 96.8 us
  other arithmetic: 189 us -> 0 us
  Pallas kernels: 0 us -> 88.4 us
  blocking collectives: 67.9 us -> 0 us
  waiting for transfers between devices: 62.4 us -> 0 us
  local copies, waits for them, and re-layouts: 68.1 us -> 7.66 us
  starting transfers between devices: 39.9 us -> 0 us
  matrix products: 33.5 us -> 0 us
    convert_element_type x5 -> x0, other arithmetic: 135 us -> none  [the longest x4 133 us: local(): shot = field.astype(jnp.bfloat16).reshape(local_runs, rows_x, plane)]
    pallas_call x0 -> x3, Pallas kernels: none -> 88.4 us  [the longest x1 45.6 us: snapshots(): pl.pallas_call(functools.partial(stencil_kernel, n_strip), out_shape=jax....]
    unnamed x1 -> x0, blocking collectives: 67.9 us -> none
    all_to_all x2 -> x0, waiting for transfers between devices: 52.3 us -> none  [exchange_in_pieces(): lax.all_to_all(share, axis, split_axis=0, concat_axis=0, tiled=True)]
    pad x4 -> x0, other arithmetic: 46.5 us -> none  [local(): padded = jnp.pad(padded, ((0, 0), (0, 0), (0, 0), (1, 1), (1, 1)))]
    squeeze x4 -> x0, local copies, waits for them, and re-layouts: 41.4 us -> none  [local(): field = advance(padded[0], padded[1])]
    dot_general x5 -> x0, matrix products: 33.5 us -> none  [the longest x1 13.8 us: local(): pred = jnp.dot(hidden_b, weight, preferred_element_type=jnp.float32)]
    ppermute x8 -> x0, starting transfers between devices: 21.3 us -> none  [the longest x4 15.8 us: padded_2(): before = lax.ppermute(last, axis, up)]
  transfers between devices with their start and end apart: 10 -> 0, of which waited for: 5 -> 0; matrix products, arithmetic and copies ran while one was open for 2% -> 0% of each run, Pallas kernels for 0% -> 0%
where the time goes in v1:
time: 97.5 us; the launch traced here: 96.8 us
  Pallas kernels  88.4 us (91%)
  local copies, waits for them, and re-layouts  7.66 us (8%)
    pallas_call x1, Pallas kernels, snapshots(): pl.pallas_call(functools.partial(stencil_kernel, n_strip), out_shape=jax....  45.6 us
    pallas_call x1, Pallas kernels, reduced(): pl.pallas_call(functools.partial(reduce_kernel, n_run, n_strip), out_shap...  29.8 us
    pallas_call x1, Pallas kernels, training(): pl.pallas_call(training_kernel, grid=(rows_x // width,), out_shape=(jax.S...  13 us
    unnamed x12, local copies, waits for them, and re-layouts  7.66 us

profile of v1, /device:TPU:1, one launch (start us, length us, event | category | flops | bytes accessed | tf_op | source)
XLA Modules:
  0.0 96.8 jit_solution(1953615763927341750)
XLA Ops:
  0.6 1.4 %copy.9.index = s32[64,6]{1,0:T(8,128)} copy(s32[64,6]{0,1:T(8,128)} %param.9) | data formatting | bytes 3072 | tf_op args[3]
  2.0 45.6 %snapshots.1.target = bf16[2,4,2,64,16,128]{5,4,3,2,1,0:T(8,128)(2,1)} custom-call(f32[6,8]{1,0:T(8,128)} %levels.3, s32[64,6]{1,0:T(8,128)} %copy.9.index, f32[64,8,256]{2,1,0:T(8,128)} %base.1, s32[64,8,256]{2,1,0:T(8,128)} %material.1), custom_call_target="tpu_custom_call" | custom-call | tf_op jit(solution)/shard_map/snapshots/pallas_call | solution.py:264
  47.7 0.0 copy-start
  47.7 2.2 %copy-done = bf16[2,4,2,64,16,128]{5,4,3,2,1,0:T(8,128)(2,1)S(1)} copy-done((bf16[2,4,2,64,16,128]{5,4,3,2,1,0:T(8,128)(2,1)S(1)}, bf16[2,4,2,64,16,128]{5,4,3,2,1,0:T(8,128)(2,1)}, u32[]{:S(2)}) %copy-start) | copy-done | bytes 4194328
  49.9 0.0 copy-start.1
  49.9 0.8 copy-done.1
  50.6 0.0 copy-start.2
  50.6 0.7 copy-done.2
  51.3 0.0 copy-start.4
  51.3 0.7 copy-done.4
  52.0 13.0 %training.1 = (bf16[512,64,128]{2,1,0:T(8,128)(2,1)}, f32[4,8,128]{2,1,0:T(8,128)S(1)}) custom-call(f32[6,8]{1,0:T(8,128)S(1)} %copy-done.4, s32[64,6]{1,0:T(8,128)S(1)} %copy-done.1, f32[8,512]{1,0:T(8,128)S(1)} %copy-done.2, bf16[512,64,128]{2,1,0:T(8,128)(2,1)} %weight.1, bf16[2,4,2,64,16,128]{5,4,3,2,1,0:T(8,128)(2,1)S(1)} %copy-done), custom_call_target="tpu_custom_call" | custom-call | tf_op jit(solution)/shard_map/training/pallas_call | solution.py:353
  65.0 0.0 copy-start.3
  65.0 0.6 copy-done.3
  65.6 29.8 %reduced.1 = f32[8,4]{1,0:T(8,128)} custom-call(f32[4,8,128]{2,1,0:T(8,128)} %copy-done.3), custom_call_target="tpu_custom_call" | custom-call | tf_op jit(solution)/shard_map/reduced/pallas_call | solution.py:440
  95.4 1.3 %copy.10 = f32[8,4]{0,1:T(4,128)} copy(f32[8,4]{1,0:T(8,128)} %reduced.1) | data formatting | bytes 256
Async XLA Ops:
  47.7 2.2 %copy-start = (bf16[2,4,2,64,16,128]{5,4,3,2,1,0:T(8,128)(2,1)S(1)}, bf16[2,4,2,64,16,128]{5,4,3,2,1,0:T(8,128)(2,1)}, u32[]{:S(2)}) copy-start(bf16[2,4,2,64,16,128]{5,4,3,2,1,0:T(8,128)(2,1)} %snapshots.1.target) | copy-start | bytes 12582916
  49.9 0.8 copy-start.1
  50.6 0.7 copy-start.2
  51.3 0.7 copy-start.4
  65.0 0.6 copy-start.3

commit v2 on v1

v2 whole, which is shorter than its diff:
```python
import functools

import jax
import jax.numpy as jnp
from jax import lax
from jax.experimental import pallas as pl
from jax.experimental.pallas import tpu as pltpu
from jax.sharding import PartitionSpec as P

STEPS = 4
TIME_STEP = 0.08
BF = jnp.bfloat16
F32 = jnp.float32
MESH = pl.DeviceIdType.MESH
GROUP = 16
LANES = 128
CHUNK = 35
WIDTH = 8


def run_values(levels_ref, index_ref):
    rows = []
    for p in range(index_ref.shape[0]):
        row = index_ref[p : p + 1, :]
        out = jnp.zeros(row.shape, F32)
        for level in range(levels_ref.shape[1]):
            out = jnp.where(row == level, levels_ref[p, level], out)
        rows.append(out)
    rows.append(jnp.zeros((8 - len(rows), index_ref.shape[1]), F32))
    return jnp.concatenate(rows, axis=0).T


def forward_kernel(n_run, n_strip, levels, index, w_in, base, material, weight, *rest):
    rows_x, nz, _ = base.shape
    units = weight.shape[0]
    batch = STEPS * index.shape[1]
    blocks = rows_x // WIDTH
    ext = rows_x + 2 * STEPS
    field = pltpu.VMEM((nz + 2, ext, 2, GROUP, LANES), BF)
    inner = pltpu.VMEM((nz, ext, 2, GROUP, LANES), BF)
    row = pltpu.VMEM((ext, 2, GROUP, LANES), BF)
    pl.run_scoped(
        functools.partial(
            forward_body, n_run, n_strip, levels, index, w_in, base, material, weight, *rest
        ),
        field, field, field, field, inner, inner, row, row, row,
        pltpu.VMEM((2, 2 * LANES, 2 * LANES), BF),
        pltpu.VMEM((blocks, units, WIDTH, LANES), BF),
        pltpu.VMEM((blocks, batch, WIDTH * LANES), BF),
        pltpu.VMEM((index.shape[1], units), F32),
        pltpu.VMEM((batch, units), F32),
        pltpu.VMEM((batch, units), BF),
        pltpu.VMEM((batch, units), F32),
    )


def forward_body(
    n_run, n_strip, levels, index, w_in, base, material, weight,
    error_out, hid_out, grad_out,
    bx, mx, shots, landed, values, partial, got_run, mid, got_strip,
    local_sem, halo_send, halo_recv, send_sem, recv_sem, w_sem, e_sem,
    s_run, r_run, s_strip, r_strip,
    u_a, u_b, k_a, k_b, cond, cond_g, tops, flux_y, flux_next, shifts,
    w_all, e_all, mixed, hid, hid_b, back,
):
    rows_x, nz, ny = base.shape
    ext = rows_x + 2 * STEPS
    run = lax.axis_index("run")
    strip = lax.axis_index("strip")
    core = lax.rem(run, 2)
    slab = lax.div(run, 2)
    partner = run + 1 - 2 * core
    right = lax.rem(strip + 1, n_strip)
    left = lax.rem(strip + n_strip - 1, n_strip)

    local = [
        pltpu.make_async_copy(src, dst.at[pl.ds(STEPS, rows_x)], local_sem.at[i])
        for i, (src, dst) in enumerate(((base, bx), (material, mx)))
    ]
    for copy in local:
        copy.start()
    blocks = rows_x // WIDTH
    fetches = [
        pltpu.make_async_copy(
            weight.at[:, pl.ds(i * WIDTH, WIDTH), :], w_all.at[i], w_sem.at[i]
        )
        for i in range(blocks)
    ]
    barrier = pltpu.get_barrier_semaphore()
    peers = [{"run": lax.rem(run + j, n_run)} for j in range(1, n_run)]
    peers += [{"strip": lax.rem(strip + j, n_strip)} for j in range(1, n_strip)]
    for where in peers:
        pl.semaphore_signal(barrier, inc=1, device_id=where, device_id_type=MESH)
    pl.semaphore_wait(barrier, n_run + n_strip - 2)
    halos = []
    for i, (src, dst) in enumerate(((base, bx), (material, mx))):
        for j, (first, to, target) in enumerate(
            ((rows_x - STEPS, 0, right), (0, STEPS + rows_x, left))
        ):
            copy = pltpu.make_async_remote_copy(
                src_ref=src.at[pl.ds(first, STEPS)],
                dst_ref=dst.at[pl.ds(to, STEPS)],
                send_sem=halo_send.at[2 * i + j],
                recv_sem=halo_recv.at[2 * i + j],
                device_id={"strip": target},
                device_id_type=MESH,
            )
            copy.start()
            halos.append(copy)

    for copy in fetches:
        copy.start()
    zero_row = jnp.zeros((2, GROUP, LANES), BF)
    vals = run_values(levels, index)
    values[...] = vals
    hidden_layer(vals, w_in, core, mixed, hid, hid_b, hid_out)

    def clear(pad):
        def body(x, carry):
            for ref in (u_a, u_b, k_a, k_b):
                ref[pad, x] = zero_row
            return carry

        lax.fori_loop(0, ext, body, 0)

    clear(0)
    clear(nz + 1)
    for copy in local:
        copy.wait()

    lane = lax.broadcasted_iota(jnp.int32, (GROUP, LANES), 1).astype(F32).astype(BF)
    first_lane = lane == jnp.asarray(0, BF)
    way = jnp.where(slab >= nz // 2, -1, 1)
    down = lax.broadcasted_iota(jnp.int32, (ny, ny), 0)
    across = lax.broadcasted_iota(jnp.int32, (ny, ny), 1)
    after = (down == across + 1).astype(F32)
    same = (down == across).astype(F32)
    shifts[0] = (after - same).astype(BF)
    shifts[1] = (after + same).astype(BF)

    def prepare(g):
        mine = values[pl.ds(pl.multiple_of(core * 2 * GROUP + g * GROUP, GROUP), GROUP), :]
        vals = [mine[:, p : p + 1] for p in range(6)]
        wide = lambda col: jnp.broadcast_to(col, (GROUP, LANES))
        kinds = [wide(0.5 * TIME_STEP * vals[m]).astype(BF) for m in range(4)]
        growth = wide(0.1 * vals[4]).astype(BF)
        start = wide(vals[5])
        return kinds, growth, start

    def fill(first, count, unroll, kinds, growth, start):
        def one(x):
            tile = bx[x]
            mats = mx[x].astype(F32)
            for z in range(nz):
                for h in range(2):
                    cut = slice(h * LANES, (h + 1) * LANES)
                    mat = jnp.broadcast_to(mats[z : z + 1, cut], (GROUP, LANES)).astype(BF)
                    c = kinds[0]
                    for m in range(1, 4):
                        c = jnp.where(mat == jnp.asarray(m, BF), kinds[m], c)
                    cg = c * growth
                    u = (jnp.broadcast_to(tile[z : z + 1, cut], (GROUP, LANES)) * start).astype(BF)
                    cond[z, x, h] = c
                    cond_g[z, x, h] = cg
                    u_a[z + 1, x, h] = u
                    k_a[z + 1, x, h] = c + cg * (u * u)

        def body(i, carry):
            for j in range(unroll):
                one(first + i * unroll + j)
            return carry

        lax.fori_loop(0, count // unroll, body, 0)

    def blank(refs, first, count):
        def body(z, carry):
            for x in range(first, first + count):
                for ref, shift in refs:
                    ref[z + shift, x] = zero_row
            return carry

        lax.fori_loop(0, nz, body, 0)

    def halves(ref, a, x):
        return [ref[a, x, 0], ref[a, x, 1]]

    def flat(block):
        count = block.shape[0] * GROUP
        sides = [block[:, h].reshape(count, LANES) for h in range(2)]
        return jnp.concatenate(sides, axis=1)

    def along_y(us, ks, zp, first, count):
        u, k = us[zp, pl.ds(first, count)], ks[zp, pl.ds(first, count)]
        rise = jnp.dot(flat(u), shifts[0], preferred_element_type=F32).astype(BF)
        pair = jnp.dot(flat(k), shifts[1], preferred_element_type=F32).astype(BF)
        face = rise * pair
        out = []
        for j in range(count):
            f = [face[j * GROUP : (j + 1) * GROUP, h * LANES : (h + 1) * LANES] for h in range(2)]
            r = [pltpu.roll(v, 1, 1) for v in f]
            out.append(
                [
                    f[0] - jnp.where(first_lane, k[j, 0] * u[j, 0], r[0]),
                    f[1] - jnp.where(first_lane, r[0], r[1]),
                ]
            )
        return out

    def keep_y(flux, first, ref):
        for j, pair in enumerate(flux):
            for h in range(2):
                ref[first + j, h] = pair[h]

    def chunks(step):
        return [(x, min(CHUNK, ext - step - x)) for x in range(step, ext - step, CHUNK)]

    def span(step):
        reach = STEPS - step
        low = jnp.maximum(slab - reach, 0)
        high = jnp.minimum(slab + reach, nz - 1)
        return jnp.where(way > 0, low, high), high - low + 1

    def start_y(us, ks):
        zp = span(1)[0] + 1
        for first, count in chunks(1):
            keep_y(along_y(us, ks, zp, first, count), first, flux_y)

    def advance(step, g, us, ks, ud, kd):
        final = step == STEPS
        begin, number = span(step)

        def one_slab(z, last):
            zp = z + 1
            after = (span(step + 1)[0] + 1) if last else zp + way
            src = (ud, kd) if last else (us, ks)
            if last and not final:
                for first, count in chunks(step):
                    keep_y(along_y(*src, after, first, count), first, flux_next)
            u, k = halves(us, zp, step), halves(ks, zp, step)
            ub, kb = halves(us, zp, step - 1), halves(ks, zp, step - 1)
            fl = [(k[h] + kb[h]) * (u[h] - ub[h]) for h in range(2)]
            for first, count in chunks(step):
                flux = None if last else along_y(*src, after, first, count)
                for x in range(first, first + count):
                    un, kn = halves(us, zp, x + 1), halves(ks, zp, x + 1)
                    uz, kz = halves(us, zp + way, x), halves(ks, zp + way, x)
                    fr = []
                    for h in range(2):
                        face = (k[h] + kn[h]) * (un[h] - u[h])
                        top = (k[h] + kz[h]) * (uz[h] - u[h])
                        total = (face - fl[h]) + (top - tops[x, h]) + flux_y[x, h]
                        new = u[h] + total
                        if final:
                            shots[h, step - 1, g, x - STEPS] = new
                        else:
                            if not last:
                                tops[x, h] = top
                            ud[zp, x, h] = new
                            kd[zp, x, h] = cond[z, x, h] + cond_g[z, x, h] * (new * new)
                        fr.append(face)
                    u, k, fl = un, kn, fr
                if flux is not None:
                    keep_y(flux, first, flux_y)
            if last and not final:
                for x in range(step, ext - step):
                    for h in range(2):
                        flux_y[x, h] = flux_next[x, h]

        def first_faces(i, carry):
            for j in range(2):
                x = step + i * 2 + j
                for h in range(2):
                    du = us[begin + 1, x, h] - us[begin + 1 - way, x, h]
                    tops[x, h] = (ks[begin + 1, x, h] + ks[begin + 1 - way, x, h]) * du
            return carry

        def slabs(i, carry):
            one_slab(begin + way * i, False)
            return carry

        lax.fori_loop(0, (ext - 2 * step) // 2, first_faces, 0)
        if not final:
            lax.fori_loop(0, number - 1, slabs, 0)
        one_slab(begin + way * (number - 1), True)
        if not final:

            @pl.when(strip == 0)
            def _():
                blank([(ud, 1)], 0, STEPS)

            @pl.when(strip == n_strip - 1)
            def _():
                blank([(ud, 1)], STEPS + rows_x, STEPS)

            def keep(i, carry):
                for j in range(8):
                    x = i * 8 + j
                    for h in range(2):
                        shots[h, step - 1, g, x] = ud[slab + 1, x + STEPS, h]
                return carry

            lax.fori_loop(0, rows_x // 8, keep, 0)

    def send(step, g):
        return pltpu.make_async_remote_copy(
            src_ref=shots.at[1 - core, step - 1, g],
            dst_ref=landed.at[step - 1, g],
            send_sem=send_sem.at[step - 1, g],
            recv_sem=recv_sem.at[step - 1, g],
            device_id={"run": partner},
            device_id_type=MESH,
        )

    def group(g, carry):
        consts = prepare(g)
        fill(STEPS, rows_x, 2, *consts)

        @pl.when(g == 0)
        def _():
            for copy in halos:
                copy.wait()

        fill(0, STEPS, 2, *consts)
        fill(STEPS + rows_x, STEPS, 2, *consts)
        everywhere = [(cond, 0), (cond_g, 0), (u_a, 1), (k_a, 1)]

        @pl.when(strip == 0)
        def _():
            blank(everywhere, 0, STEPS)

        @pl.when(strip == n_strip - 1)
        def _():
            blank(everywhere, STEPS + rows_x, STEPS)

        start_y(u_a, k_a)
        pairs = [(u_a, k_a), (u_b, k_b)]
        for step in range(1, STEPS + 1):
            src, dst = pairs[(step - 1) % 2], pairs[step % 2]
            advance(step, g, *src, *dst)
            send(step, g).start()
        return carry

    lax.fori_loop(0, 2, group, 0)
    for copy in fetches:
        copy.wait()
    back[...] = jnp.zeros_like(back)
    for g in range(2):
        for step in range(1, STEPS + 1):
            send(step, g).wait()

    batch = hid.shape[0]

    def put(i):
        return pltpu.make_async_copy(e_all.at[i], error_out.at[i], e_sem.at[i])

    def train(i, carry):
        w = jnp.swapaxes(w_all[i], 0, 1)
        w = jnp.concatenate([w[x] for x in range(WIDTH)], axis=1)
        pred = jnp.dot(hid_b[...], w, preferred_element_type=F32)
        cuts = []
        for x in range(WIDTH):
            at = i * WIDTH + x
            tiles = [shots[core, t, g, at] for t in range(STEPS) for g in range(2)]
            tiles += [landed[t, g, at] for t in range(STEPS) for g in range(2)]
            cuts.append(jnp.concatenate(tiles, axis=0))
        goal = jnp.concatenate(cuts, axis=1)
        error = ((pred - goal.astype(F32)) * (batch ** -0.5)).astype(BF)
        e_all[i] = error
        put(i).start()
        back[...] += lax.dot_general(
            error, w, (((1,), (1,)), ((), ())), preferred_element_type=F32
        )
        return carry

    lax.fori_loop(0, blocks, train, 0)
    input_gradient(values, core, hid, back, partial)
    reduce_scatter(
        n_run, n_strip, partial, grad_out, got_run, mid, got_strip, s_run, r_run, s_strip, r_strip
    )
    for i in range(blocks):
        put(i).wait()


def hidden_layer(vals, w_in, core, mixed, hid, hid_b, hid_out):
    half = 2 * GROUP
    total = vals[:, 0:1] * w_in[0:1, :]
    for p in range(1, 6):
        total = total + vals[:, p : p + 1] * w_in[p : p + 1, :]
    mixed[...] = total
    for part in range(2):
        owner = core if part == 0 else 1 - core
        rows = mixed[pl.ds(pl.multiple_of(owner * half, half), half), :]
        for t in range(STEPS):
            pre = rows + ((t + 1.0) / STEPS) * w_in[6:7, :] + w_in[7:8, :]
            hid[pl.ds((part * STEPS + t) * half, half), :] = jnp.tanh(pre)
    hid_b[...] = hid[...].astype(BF)
    hid_out[...] = hid[...].T.astype(BF)


def input_gradient(values, core, hid, back, partial):
    half = 2 * GROUP
    h = hid[...]
    slope = back[...] * (1.0 - h * h)
    steps = [
        [slope[(part * STEPS + t) * half : (part * STEPS + t + 1) * half] for t in range(STEPS)]
        for part in range(2)
    ]
    runs = [p[0] + p[1] + p[2] + p[3] for p in steps]
    vals = [
        values[pl.ds(pl.multiple_of((core if part == 0 else 1 - core) * half, half), half), :]
        for part in range(2)
    ]
    rows = []
    for p in range(6):
        both = vals[0][:, p : p + 1] * runs[0] + vals[1][:, p : p + 1] * runs[1]
        rows.append(jnp.sum(both, axis=0, keepdims=True))
    timed = sum(((t + 1.0) / STEPS) * (steps[0][t] + steps[1][t]) for t in range(STEPS))
    rows.append(jnp.sum(timed, axis=0, keepdims=True))
    rows.append(jnp.sum(runs[0] + runs[1], axis=0, keepdims=True))
    full = jnp.concatenate(rows, axis=0)
    for q in range(partial.shape[0]):
        partial[q] = full[:, q * LANES : (q + 1) * LANES]


def reduce_scatter(
    n_run, n_strip, partial, out, got_run, mid, got_strip, s_run, r_run, s_strip, r_strip
):
    run = lax.axis_index("run")
    strip = lax.axis_index("strip")
    units = partial.shape[0] * LANES
    keep = units // (n_run * n_strip)
    per = LANES // (n_strip * keep)
    copies = []
    for j in range(1, n_run):
        to = lax.rem(run + j, n_run)
        copies.append(
            pltpu.make_async_remote_copy(
                src_ref=partial.at[lax.div(to, per)],
                dst_ref=got_run.at[j - 1],
                send_sem=s_run.at[j - 1],
                recv_sem=r_run.at[j - 1],
                device_id={"run": to},
                device_id_type=MESH,
            )
        )
        copies[-1].start()
    total = partial[lax.div(run, per)]
    for j in range(n_run - 1):
        copies[j].wait_recv()
        total = total + got_run[j]
    mid[...] = total
    more = []
    for j in range(1, n_strip):
        to = lax.rem(strip + j, n_strip)
        more.append(
            pltpu.make_async_remote_copy(
                src_ref=mid,
                dst_ref=got_strip.at[j - 1],
                send_sem=s_strip.at[j - 1],
                recv_sem=r_strip.at[j - 1],
                device_id={"strip": to},
                device_id_type=MESH,
            )
        )
        more[-1].start()
    for j in range(n_strip - 1):
        more[j].wait_recv()
        total = total + got_strip[j]
    for copy in copies + more:
        copy.wait_send()
    at = lax.rem(run, per) * (n_strip * keep) + strip * keep
    out[...] = pltpu.roll(total, lax.rem(LANES - at, LANES), 1)


def forward(levels, index, w_in, base, material, weight, n_run, n_strip):
    rows_x, nz, ny = base.shape
    units = weight.shape[0]
    batch = STEPS * index.shape[1]
    blocks = rows_x // WIDTH
    ext = rows_x + 2 * STEPS
    hbm = pl.BlockSpec(memory_space=pl.ANY)
    vmem = pl.BlockSpec(memory_space=pltpu.VMEM)
    dma = pltpu.SemaphoreType.DMA
    return pl.pallas_call(
        functools.partial(forward_kernel, n_run, n_strip),
        out_shape=(
            jax.ShapeDtypeStruct((blocks, batch, WIDTH * LANES), BF),
            jax.ShapeDtypeStruct((units, batch), BF),
            jax.ShapeDtypeStruct((8, LANES), F32),
        ),
        in_specs=[pl.BlockSpec(memory_space=pltpu.SMEM), vmem, vmem, hbm, hbm, hbm],
        out_specs=(hbm, vmem, vmem),
        scratch_shapes=[
            pltpu.VMEM((ext, nz, ny), F32),
            pltpu.VMEM((ext, nz, ny), jnp.int32),
            pltpu.VMEM((2, STEPS, 2, rows_x, GROUP, LANES), BF),
            pltpu.VMEM((STEPS, 2, rows_x, GROUP, LANES), BF),
            pltpu.VMEM((index.shape[1], 8), F32),
            pltpu.VMEM((units // LANES, 8, LANES), F32),
            pltpu.VMEM((n_run - 1, 8, LANES), F32),
            pltpu.VMEM((8, LANES), F32),
            pltpu.VMEM((n_strip - 1, 8, LANES), F32),
            dma((2,)), dma((4,)), dma((4,)), dma((STEPS, 2)), dma((STEPS, 2)),
            dma((blocks,)), dma((blocks,)),
            dma((n_run - 1,)), dma((n_run - 1,)), dma((n_strip - 1,)), dma((n_strip - 1,)),
        ],
        compiler_params=pltpu.CompilerParams(
            collective_id=0, has_side_effects=True, vmem_limit_bytes=63 * 1024 * 1024
        ),
        name="forward",
    )(levels, index, w_in, base, material, weight)


def output_kernel(hid, total, error, grad, turned, e_all, g_all, e_sem, g_sem):
    blocks = e_all.shape[0]
    fetches = [pltpu.make_async_copy(error.at[i], e_all.at[i], e_sem.at[i]) for i in range(blocks)]
    for copy in fetches:
        copy.start()
    turned[...] = total[...].T[: turned.shape[0]]
    puts = []
    for i in range(blocks):
        fetches[i].wait()
        g = jnp.dot(hid[...], e_all[i], preferred_element_type=F32).astype(BF)
        g = jnp.stack([g[:, x * LANES : (x + 1) * LANES] for x in range(WIDTH)], axis=0)
        g_all[i] = jnp.swapaxes(g, 0, 1)
        puts.append(
            pltpu.make_async_copy(
                g_all.at[i], grad.at[:, pl.ds(i * WIDTH, WIDTH), :], g_sem.at[i]
            )
        )
        puts[-1].start()
    for copy in puts:
        copy.wait()


def output_gradient(hid, total, error, keep):
    units, batch = hid.shape
    blocks = error.shape[0]
    hbm = pl.BlockSpec(memory_space=pl.ANY)
    vmem = pl.BlockSpec(memory_space=pltpu.VMEM)
    return pl.pallas_call(
        output_kernel,
        out_shape=(
            jax.ShapeDtypeStruct((units, blocks * WIDTH, LANES), BF),
            jax.ShapeDtypeStruct((keep, 8), F32),
        ),
        in_specs=[vmem, vmem, hbm],
        out_specs=(hbm, vmem),
        scratch_shapes=[
            pltpu.VMEM(error.shape, BF),
            pltpu.VMEM((blocks, units, WIDTH, LANES), BF),
            pltpu.SemaphoreType.DMA((blocks,)),
            pltpu.SemaphoreType.DMA((blocks,)),
        ],
        compiler_params=pltpu.CompilerParams(vmem_limit_bytes=63 * 1024 * 1024),
        name="output_gradient",
    )(hid, total, error)


def solution(mesh):
    n_run, n_strip = mesh.shape["run"], mesh.shape["strip"]

    def local(base_field, material_map, param_levels, param_index, w_input, w_output):
        error, hid, total = forward(
            param_levels, param_index.T, w_input, base_field, material_map, w_output, n_run, n_strip
        )
        keep = w_output.shape[0] // (n_run * n_strip)
        grad_output, turned = output_gradient(hid, total, error, keep)
        return grad_output, turned.T

    placed = (
        P("strip", None, None),
        P("strip", None, None),
        P(),
        P(),
        P(),
        P(None, "strip", "run"),
    )
    return jax.shard_map(
        local,
        mesh=mesh,
        in_specs=placed,
        out_specs=(P(None, "strip", "run"), P(None, ("run", "strip"))),
        check_vma=False,
    )
```

time: 97.5 us -> 66.5 us (0.68)
  Pallas kernels: 88.4 us -> 65.6 us
  local copies, waits for them, and re-layouts: 7.66 us -> 0 us
    pallas_call x3 -> x2, Pallas kernels: 88.4 us -> 65.6 us  [the longest x1 57.4 us: forward(): pl.pallas_call(functools.partial(forward_kernel, n_run, n_strip), out_sha...]
    unnamed x12 -> x0, local copies, waits for them, and re-layouts: 7.66 us -> none
where the time goes in v2:
time: 66.5 us; the launch traced here: 66.3 us
  Pallas kernels  65.6 us (99%)
    pallas_call x1, Pallas kernels, forward(): pl.pallas_call(functools.partial(forward_kernel, n_run, n_strip), out_sha...  57.4 us
    pallas_call x1, Pallas kernels, output_gradient(): pl.pallas_call(output_kernel, out_shape=(jax.ShapeDtypeStruct((units, blo...  8.23 us

profile of v2, /device:TPU:1, one launch (start us, length us, event | category | flops | bytes accessed | tf_op | source)
XLA Modules:
  0.0 66.3 jit_solution(10059694434303717378)
XLA Ops:
  0.6 57.4 %forward.1 = (bf16[8,256,1024]{2,1,0:T(8,128)(2,1)}, bf16[512,256]{1,0:T(8,128)(2,1)}, f32[8,128]{1,0:T(8,128)}) custom-call(f32[6,8]{1,0:T(8,128)} %levels.1, s32[6,64]{1,0:T(8,128)} %bitcast.2, f32[8,512]{1,0:T(8,128)} %w_in.1, f32[64,8,256]{2,1,0:T(8,128)} %base.1, s32[64,8,256]{2,1,0:T(8,128)} %material.1, bf16[512,64,128]{2,1,0:T(8,128)(2,1)} %weight.1), custom_call_target="tpu_custom_call" | custom-call | tf_op jit(solution)/shard_map/forward/pallas_call | solution.py:484
  58.1 8.2 %output_gradient.1 = (bf16[512,64,128]{2,1,0:T(8,128)(2,1)}, f32[4,8]{1,0:T(4,128)}) custom-call(bf16[512,256]{1,0:T(8,128)(2,1)} %get-tuple-element.7.hid, f32[8,128]{1,0:T(8,128)} %get-tuple-element.8.total, bf16[8,256,1024]{2,1,0:T(8,128)(2,1)} %get-tuple-element.9.error), custom_call_target="tpu_custom_call" | custom-call | tf_op jit(solution)/shard_map/output_gradient/pallas_call | solution.py:541

commit v3 on v2

--- a/solution.py
+++ b/solution.py
@@ -16,6 +16,7 @@
 LANES = 128
 CHUNK = 35
 WIDTH = 8
+TURN = 2
 
 
 def run_values(levels_ref, index_ref):
@@ -24,16 +25,16 @@
         row = index_ref[p : p + 1, :]
         out = jnp.zeros(row.shape, F32)
         for level in range(levels_ref.shape[1]):
-            out = jnp.where(row == level, levels_ref[p, level], out)
+            out = jnp.where(row == level, levels_ref[p : p + 1, level : level + 1], out)
         rows.append(out)
     rows.append(jnp.zeros((8 - len(rows), index_ref.shape[1]), F32))
     return jnp.concatenate(rows, axis=0).T
 
 
-def forward_kernel(n_run, n_strip, levels, index, w_in, base, material, weight, *rest):
+def forward_kernel(n_run, n_strip, levels_in, index_in, w_in_in, base, material, weight, *rest):
     rows_x, nz, _ = base.shape
     units = weight.shape[0]
-    batch = STEPS * index.shape[1]
+    batch = STEPS * index_in.shape[1]
     blocks = rows_x // WIDTH
     ext = rows_x + 2 * STEPS
     field = pltpu.VMEM((nz + 2, ext, 2, GROUP, LANES), BF)
@@ -41,27 +42,31 @@
     row = pltpu.VMEM((ext, 2, GROUP, LANES), BF)
     pl.run_scoped(
         functools.partial(
-            forward_body, n_run, n_strip, levels, index, w_in, base, material, weight, *rest
+            forward_body, n_run, n_strip, levels_in, index_in, w_in_in, base, material, weight, *rest
         ),
         field, field, field, field, inner, inner, row, row, row,
         pltpu.VMEM((2, 2 * LANES, 2 * LANES), BF),
         pltpu.VMEM((blocks, units, WIDTH, LANES), BF),
         pltpu.VMEM((blocks, batch, WIDTH * LANES), BF),
-        pltpu.VMEM((index.shape[1], units), F32),
+        pltpu.VMEM((index_in.shape[1], units), F32),
         pltpu.VMEM((batch, units), F32),
         pltpu.VMEM((batch, units), BF),
+        pltpu.VMEM((units, batch), BF),
         pltpu.VMEM((batch, units), F32),
+        pltpu.VMEM(levels_in.shape, F32),
+        pltpu.VMEM(index_in.shape, jnp.int32),
+        pltpu.VMEM(w_in_in.shape, F32),
     )
 
 
 def forward_body(
-    n_run, n_strip, levels, index, w_in, base, material, weight,
+    n_run, n_strip, levels_in, index_in, w_in_in, base, material, weight,
     error_out, hid_out, grad_out,
     bx, mx, shots, landed, values, partial, got_run, mid, got_strip,
-    local_sem, halo_send, halo_recv, send_sem, recv_sem, w_sem, e_sem,
+    local_sem, small_sem, halo_send, halo_recv, send_sem, recv_sem, w_sem, e_sem,
     s_run, r_run, s_strip, r_strip,
     u_a, u_b, k_a, k_b, cond, cond_g, tops, flux_y, flux_next, shifts,
-    w_all, e_all, mixed, hid, hid_b, back,
+    w_all, e_all, mixed, hid, hid_b, hid_t, back, levels, index, w_in,
 ):
     rows_x, nz, ny = base.shape
     ext = rows_x + 2 * STEPS
@@ -77,7 +82,11 @@
         pltpu.make_async_copy(src, dst.at[pl.ds(STEPS, rows_x)], local_sem.at[i])
         for i, (src, dst) in enumerate(((base, bx), (material, mx)))
     ]
-    for copy in local:
+    small = [
+        pltpu.make_async_copy(src, dst, small_sem.at[i])
+        for i, (src, dst) in enumerate(((levels_in, levels), (index_in, index), (w_in_in, w_in)))
+    ]
+    for copy in small + local:
         copy.start()
     blocks = rows_x // WIDTH
     fetches = [
@@ -91,29 +100,23 @@
     peers += [{"strip": lax.rem(strip + j, n_strip)} for j in range(1, n_strip)]
     for where in peers:
         pl.semaphore_signal(barrier, inc=1, device_id=where, device_id_type=MESH)
-    pl.semaphore_wait(barrier, n_run + n_strip - 2)
     halos = []
     for i, (src, dst) in enumerate(((base, bx), (material, mx))):
         for j, (first, to, target) in enumerate(
             ((rows_x - STEPS, 0, right), (0, STEPS + rows_x, left))
         ):
-            copy = pltpu.make_async_remote_copy(
-                src_ref=src.at[pl.ds(first, STEPS)],
-                dst_ref=dst.at[pl.ds(to, STEPS)],
-                send_sem=halo_send.at[2 * i + j],
-                recv_sem=halo_recv.at[2 * i + j],
-                device_id={"strip": target},
-                device_id_type=MESH,
+            halos.append(
+                pltpu.make_async_remote_copy(
+                    src_ref=src.at[pl.ds(first, STEPS)],
+                    dst_ref=dst.at[pl.ds(to, STEPS)],
+                    send_sem=halo_send.at[2 * i + j],
+                    recv_sem=halo_recv.at[2 * i + j],
+                    device_id={"strip": target},
+                    device_id_type=MESH,
+                )
             )
-            copy.start()
-            halos.append(copy)
-
-    for copy in fetches:
-        copy.start()
+    hid_put = pltpu.make_async_copy(hid_t, hid_out, small_sem.at[3])
     zero_row = jnp.zeros((2, GROUP, LANES), BF)
-    vals = run_values(levels, index)
-    values[...] = vals
-    hidden_layer(vals, w_in, core, mixed, hid, hid_b, hid_out)
 
     def clear(pad):
         def body(x, carry):
@@ -125,8 +128,10 @@
 
     clear(0)
     clear(nz + 1)
-    for copy in local:
+    for copy in small:
         copy.wait()
+    vals = run_values(levels, index)
+    values[...] = vals
 
     lane = lax.broadcasted_iota(jnp.int32, (GROUP, LANES), 1).astype(F32).astype(BF)
     first_lane = lane == jnp.asarray(0, BF)
@@ -312,16 +317,10 @@
         )
 
     def group(g, carry):
-        consts = prepare(g)
-        fill(STEPS, rows_x, 2, *consts)
-
-        @pl.when(g == 0)
+        @pl.when(g > 0)
         def _():
-            for copy in halos:
-                copy.wait()
-
-        fill(0, STEPS, 2, *consts)
-        fill(STEPS + rows_x, STEPS, 2, *consts)
+            fill(0, ext, 2, *prepare(g))
+
         everywhere = [(cond, 0), (cond_g, 0), (u_a, 1), (k_a, 1)]
 
         @pl.when(strip == 0)
@@ -340,6 +339,20 @@
             send(step, g).start()
         return carry
 
+    consts = prepare(0)
+    for copy in local:
+        copy.wait()
+    fill(STEPS, rows_x // 2, 2, *consts)
+    pl.semaphore_wait(barrier, n_run + n_strip - 2)
+    for copy in halos + fetches:
+        copy.start()
+    fill(STEPS + rows_x // 2, rows_x // 2, 2, *consts)
+    hidden_layer(vals, w_in, core, mixed, hid, hid_b, hid_t)
+    hid_put.start()
+    for copy in halos:
+        copy.wait()
+    fill(0, STEPS, 2, *consts)
+    fill(STEPS + rows_x, STEPS, 2, *consts)
     lax.fori_loop(0, 2, group, 0)
     for copy in fetches:
         copy.wait()
@@ -353,7 +366,7 @@
     def put(i):
         return pltpu.make_async_copy(e_all.at[i], error_out.at[i], e_sem.at[i])
 
-    def train(i, carry):
+    def train(i):
         w = jnp.swapaxes(w_all[i], 0, 1)
         w = jnp.concatenate([w[x] for x in range(WIDTH)], axis=1)
         pred = jnp.dot(hid_b[...], w, preferred_element_type=F32)
@@ -367,21 +380,23 @@
         error = ((pred - goal.astype(F32)) * (batch ** -0.5)).astype(BF)
         e_all[i] = error
         put(i).start()
-        back[...] += lax.dot_general(
-            error, w, (((1,), (1,)), ((), ())), preferred_element_type=F32
-        )
+        return lax.dot_general(error, w, (((1,), (1,)), ((), ())), preferred_element_type=F32)
+
+    def several(i, carry):
+        back[...] += sum(train(i * TURN + j) for j in range(TURN))
         return carry
 
-    lax.fori_loop(0, blocks, train, 0)
+    lax.fori_loop(0, blocks // TURN, several, 0)
     input_gradient(values, core, hid, back, partial)
     reduce_scatter(
         n_run, n_strip, partial, grad_out, got_run, mid, got_strip, s_run, r_run, s_strip, r_strip
     )
+    hid_put.wait()
     for i in range(blocks):
         put(i).wait()
 
 
-def hidden_layer(vals, w_in, core, mixed, hid, hid_b, hid_out):
+def hidden_layer(vals, w_in, core, mixed, hid, hid_b, hid_t):
     half = 2 * GROUP
     total = vals[:, 0:1] * w_in[0:1, :]
     for p in range(1, 6):
@@ -394,7 +409,7 @@
             pre = rows + ((t + 1.0) / STEPS) * w_in[6:7, :] + w_in[7:8, :]
             hid[pl.ds((part * STEPS + t) * half, half), :] = jnp.tanh(pre)
     hid_b[...] = hid[...].astype(BF)
-    hid_out[...] = hid[...].T.astype(BF)
+    hid_t[...] = hid[...].T.astype(BF)
 
 
 def input_gradient(values, core, hid, back, partial):
@@ -488,8 +503,8 @@
             jax.ShapeDtypeStruct((units, batch), BF),
             jax.ShapeDtypeStruct((8, LANES), F32),
         ),
-        in_specs=[pl.BlockSpec(memory_space=pltpu.SMEM), vmem, vmem, hbm, hbm, hbm],
-        out_specs=(hbm, vmem, vmem),
+        in_specs=[hbm] * 6,
+        out_specs=(hbm, hbm, vmem),
         scratch_shapes=[
             pltpu.VMEM((ext, nz, ny), F32),
             pltpu.VMEM((ext, nz, ny), jnp.int32),
@@ -500,7 +515,7 @@
             pltpu.VMEM((n_run - 1, 8, LANES), F32),
             pltpu.VMEM((8, LANES), F32),
             pltpu.VMEM((n_strip - 1, 8, LANES), F32),
-            dma((2,)), dma((4,)), dma((4,)), dma((STEPS, 2)), dma((STEPS, 2)),
+            dma((2,)), dma((4,)), dma((4,)), dma((4,)), dma((STEPS, 2)), dma((STEPS, 2)),
             dma((blocks,)), dma((blocks,)),
             dma((n_run - 1,)), dma((n_run - 1,)), dma((n_strip - 1,)), dma((n_strip - 1,)),
         ],
@@ -511,13 +526,15 @@
     )(levels, index, w_in, base, material, weight)
 
 
-def output_kernel(hid, total, error, grad, turned, e_all, g_all, e_sem, g_sem):
+def output_kernel(hid_in, total, error, grad, turned, hid, e_all, g_all, h_sem, e_sem, g_sem):
     blocks = e_all.shape[0]
     fetches = [pltpu.make_async_copy(error.at[i], e_all.at[i], e_sem.at[i]) for i in range(blocks)]
-    for copy in fetches:
+    first = pltpu.make_async_copy(hid_in, hid, h_sem)
+    for copy in [first] + fetches:
         copy.start()
     turned[...] = total[...].T[: turned.shape[0]]
     puts = []
+    first.wait()
     for i in range(blocks):
         fetches[i].wait()
         g = jnp.dot(hid[...], e_all[i], preferred_element_type=F32).astype(BF)
@@ -544,11 +561,13 @@
             jax.ShapeDtypeStruct((units, blocks * WIDTH, LANES), BF),
             jax.ShapeDtypeStruct((keep, 8), F32),
         ),
-        in_specs=[vmem, vmem, hbm],
+        in_specs=[hbm, vmem, hbm],
         out_specs=(hbm, vmem),
         scratch_shapes=[
+            pltpu.VMEM(hid.shape, BF),
             pltpu.VMEM(error.shape, BF),
             pltpu.VMEM((blocks, units, WIDTH, LANES), BF),
+            pltpu.SemaphoreType.DMA,
             pltpu.SemaphoreType.DMA((blocks,)),
             pltpu.SemaphoreType.DMA((blocks,)),
         ],

time: 66.5 us -> 64.5 us (0.970)
  Pallas kernels: 65.6 us -> 63.7 us
    pallas_call x1, Pallas kernels: 57.4 us -> 54.7 us  [forward(): pl.pallas_call(functools.partial(forward_kernel, n_run, n_strip), out_sha...]
    pallas_call x1, Pallas kernels: 8.23 us -> 8.97 us  [output_gradient(): pl.pallas_call(output_kernel, out_shape=(jax.ShapeDtypeStruct((units, blo...]
where the time goes in v3:
time: 64.5 us; the launch traced here: 64.3 us
  Pallas kernels  63.7 us (99%)
    pallas_call x1, Pallas kernels, forward(): pl.pallas_call(functools.partial(forward_kernel, n_run, n_strip), out_sha...  54.7 us
    pallas_call x1, Pallas kernels, output_gradient(): pl.pallas_call(output_kernel, out_shape=(jax.ShapeDtypeStruct((units, blo...  8.97 us

profile of v3, /device:TPU:1, one launch (start us, length us, event | category | flops | bytes accessed | tf_op | source)
XLA Modules:
  0.0 64.3 jit_solution(15646639280298791604)
XLA Ops:
  0.6 54.7 %forward.1 = (bf16[8,256,1024]{2,1,0:T(8,128)(2,1)}, bf16[512,256]{1,0:T(8,128)(2,1)}, f32[8,128]{1,0:T(8,128)}) custom-call(f32[6,8]{1,0:T(8,128)} %levels_in.1, s32[6,64]{1,0:T(8,128)} %bitcast.2, f32[8,512]{1,0:T(8,128)} %w_in_in.1, f32[64,8,256]{2,1,0:T(8,128)} %base.1, s32[64,8,256]{2,1,0:T(8,128)} %material.1, bf16[512,64,128]{2,1,0:T(8,128)(2,1)} %weight.1), custom_call_target="tpu_custom_call" | custom-call | tf_op jit(solution)/shard_map/forward/pallas_call | solution.py:499
  55.4 9.0 %output_gradient.1 = (bf16[512,64,128]{2,1,0:T(8,128)(2,1)}, f32[4,8]{1,0:T(4,128)}) custom-call(bf16[512,256]{1,0:T(8,128)(2,1)} %get-tuple-element.7.hid_in, f32[8,128]{1,0:T(8,128)} %get-tuple-element.8.total, bf16[8,256,1024]{2,1,0:T(8,128)(2,1)} %get-tuple-element.9.error), custom_call_target="tpu_custom_call" | custom-call | tf_op jit(solution)/shard_map/output_gradient/pallas_call | solution.py:558

commit v4 on v3

--- a/solution.py
+++ b/solution.py
@@ -101,13 +101,13 @@
     for where in peers:
         pl.semaphore_signal(barrier, inc=1, device_id=where, device_id_type=MESH)
     halos = []
-    for i, (src, dst) in enumerate(((base, bx), (material, mx))):
+    for i, dst in enumerate((bx, mx)):
         for j, (first, to, target) in enumerate(
-            ((rows_x - STEPS, 0, right), (0, STEPS + rows_x, left))
+            ((rows_x, 0, right), (STEPS, STEPS + rows_x, left))
         ):
             halos.append(
                 pltpu.make_async_remote_copy(
-                    src_ref=src.at[pl.ds(first, STEPS)],
+                    src_ref=dst.at[pl.ds(first, STEPS)],
                     dst_ref=dst.at[pl.ds(to, STEPS)],
                     send_sem=halo_send.at[2 * i + j],
                     recv_sem=halo_recv.at[2 * i + j],
@@ -130,6 +130,8 @@
     clear(nz + 1)
     for copy in small:
         copy.wait()
+    for copy in fetches:
+        copy.start()
     vals = run_values(levels, index)
     values[...] = vals
 
@@ -216,8 +218,19 @@
             for h in range(2):
                 ref[first + j, h] = pair[h]
 
-    def chunks(step):
-        return [(x, min(CHUNK, ext - step - x)) for x in range(step, ext - step, CHUNK)]
+    def pieces(step, part):
+        if part == "inner":
+            return [(STEPS + step, rows_x - 2 * step)]
+        if part == "edge":
+            return [(step, STEPS), (ext - step - STEPS, STEPS)]
+        return [(step, ext - 2 * step)]
+
+    def chunks(step, part):
+        return [
+            (x, min(CHUNK, first + count - x), x == first)
+            for first, count in pieces(step, part)
+            for x in range(first, first + count, CHUNK)
+        ]
 
     def span(step):
         reach = STEPS - step
@@ -225,12 +238,12 @@
         high = jnp.minimum(slab + reach, nz - 1)
         return jnp.where(way > 0, low, high), high - low + 1
 
-    def start_y(us, ks):
+    def start_y(us, ks, part):
         zp = span(1)[0] + 1
-        for first, count in chunks(1):
+        for first, count, _ in chunks(1, part):
             keep_y(along_y(us, ks, zp, first, count), first, flux_y)
 
-    def advance(step, g, us, ks, ud, kd):
+    def advance(step, g, us, ks, ud, kd, part):
         final = step == STEPS
         begin, number = span(step)
 
@@ -239,12 +252,13 @@
             after = (span(step + 1)[0] + 1) if last else zp + way
             src = (ud, kd) if last else (us, ks)
             if last and not final:
-                for first, count in chunks(step):
+                for first, count, _ in chunks(step + 1, part):
                     keep_y(along_y(*src, after, first, count), first, flux_next)
-            u, k = halves(us, zp, step), halves(ks, zp, step)
-            ub, kb = halves(us, zp, step - 1), halves(ks, zp, step - 1)
-            fl = [(k[h] + kb[h]) * (u[h] - ub[h]) for h in range(2)]
-            for first, count in chunks(step):
+            for first, count, fresh in chunks(step, part):
+                if fresh:
+                    u, k = halves(us, zp, first), halves(ks, zp, first)
+                    ub, kb = halves(us, zp, first - 1), halves(ks, zp, first - 1)
+                    fl = [(k[h] + kb[h]) * (u[h] - ub[h]) for h in range(2)]
                 flux = None if last else along_y(*src, after, first, count)
                 for x in range(first, first + count):
                     un, kn = halves(us, zp, x + 1), halves(ks, zp, x + 1)
@@ -267,13 +281,14 @@
                 if flux is not None:
                     keep_y(flux, first, flux_y)
             if last and not final:
-                for x in range(step, ext - step):
-                    for h in range(2):
-                        flux_y[x, h] = flux_next[x, h]
-
-        def first_faces(i, carry):
+                for first, count in pieces(step + 1, part):
+                    for x in range(first, first + count):
+                        for h in range(2):
+                            flux_y[x, h] = flux_next[x, h]
+
+        def first_faces(first, i, carry):
             for j in range(2):
-                x = step + i * 2 + j
+                x = first + i * 2 + j
                 for h in range(2):
                     du = us[begin + 1, x, h] - us[begin + 1 - way, x, h]
                     tops[x, h] = (ks[begin + 1, x, h] + ks[begin + 1 - way, x, h]) * du
@@ -283,11 +298,14 @@
             one_slab(begin + way * i, False)
             return carry
 
-        lax.fori_loop(0, (ext - 2 * step) // 2, first_faces, 0)
+        for first, count in pieces(step, part):
+            lax.fori_loop(0, count // 2, functools.partial(first_faces, first), 0)
         if not final:
             lax.fori_loop(0, number - 1, slabs, 0)
         one_slab(begin + way * (number - 1), True)
-        if not final:
+        if final:
+            return
+        if part != "inner":
 
             @pl.when(strip == 0)
             def _():
@@ -297,14 +315,23 @@
             def _():
                 blank([(ud, 1)], STEPS + rows_x, STEPS)
 
-            def keep(i, carry):
-                for j in range(8):
-                    x = i * 8 + j
-                    for h in range(2):
-                        shots[h, step - 1, g, x] = ud[slab + 1, x + STEPS, h]
-                return carry
-
-            lax.fori_loop(0, rows_x // 8, keep, 0)
+        def keep(x):
+            for h in range(2):
+                shots[h, step - 1, g, x - STEPS] = ud[slab + 1, x, h]
+
+        if part == "edge":
+            for j in range(step):
+                keep(STEPS + j)
+                keep(STEPS + rows_x - 1 - j)
+            return
+        first, count = (STEPS, rows_x) if part == "full" else pieces(step, part)[0]
+
+        def several_rows(i, carry):
+            for j in range(2):
+                keep(first + i * 2 + j)
+            return carry
+
+        lax.fori_loop(0, count // 2, several_rows, 0)
 
     def send(step, g):
         return pltpu.make_async_remote_copy(
@@ -316,43 +343,59 @@
             device_id_type=MESH,
         )
 
+    fields = [(u_a, k_a), (u_b, k_b)]
+    everywhere = [(cond, 0), (cond_g, 0), (u_a, 1), (k_a, 1)]
+
+    def all_edges():
+        @pl.when(strip == 0)
+        def _():
+            blank(everywhere, 0, STEPS)
+
+        @pl.when(strip == n_strip - 1)
+        def _():
+            blank(everywhere, STEPS + rows_x, STEPS)
+
+    def move(step, g, part):
+        advance(step, g, *fields[(step - 1) % 2], *fields[step % 2], part)
+
+    consts = prepare(0)
+    for copy in local:
+        copy.wait()
+    fill(STEPS, rows_x, 2, *consts)
+    hidden_layer(vals, w_in, core, mixed, hid, hid_b, hid_t)
+    hid_put.start()
+
     def group(g, carry):
         @pl.when(g > 0)
         def _():
             fill(0, ext, 2, *prepare(g))
 
-        everywhere = [(cond, 0), (cond_g, 0), (u_a, 1), (k_a, 1)]
-
-        @pl.when(strip == 0)
+        start_y(u_a, k_a, "inner")
+        move(1, g, "inner")
+
+        @pl.when(g == 0)
         def _():
-            blank(everywhere, 0, STEPS)
-
-        @pl.when(strip == n_strip - 1)
+            pl.semaphore_wait(barrier, n_run + n_strip - 2)
+            for copy in halos:
+                copy.start()
+
+        for step in range(2, STEPS + 1):
+            move(step, g, "inner")
+
+        @pl.when(g == 0)
         def _():
-            blank(everywhere, STEPS + rows_x, STEPS)
-
-        start_y(u_a, k_a)
-        pairs = [(u_a, k_a), (u_b, k_b)]
+            for copy in halos:
+                copy.wait()
+            fill(0, STEPS, 1, *prepare(g))
+            fill(STEPS + rows_x, STEPS, 1, *prepare(g))
+
+        all_edges()
+        start_y(u_a, k_a, "edge")
         for step in range(1, STEPS + 1):
-            src, dst = pairs[(step - 1) % 2], pairs[step % 2]
-            advance(step, g, *src, *dst)
+            move(step, g, "edge")
             send(step, g).start()
         return carry
 
-    consts = prepare(0)
-    for copy in local:
-        copy.wait()
-    fill(STEPS, rows_x // 2, 2, *consts)
-    pl.semaphore_wait(barrier, n_run + n_strip - 2)
-    for copy in halos + fetches:
-        copy.start()
-    fill(STEPS + rows_x // 2, rows_x // 2, 2, *consts)
-    hidden_layer(vals, w_in, core, mixed, hid, hid_b, hid_t)
-    hid_put.start()
-    for copy in halos:
-        copy.wait()
-    fill(0, STEPS, 2, *consts)
-    fill(STEPS + rows_x, STEPS, 2, *consts)
     lax.fori_loop(0, 2, group, 0)
     for copy in fetches:
         copy.wait()
@@ -526,15 +569,13 @@
     )(levels, index, w_in, base, material, weight)
 
 
-def output_kernel(hid_in, total, error, grad, turned, hid, e_all, g_all, h_sem, e_sem, g_sem):
+def output_kernel(hid, total, error, grad, turned, e_all, g_all, e_sem, g_sem):
     blocks = e_all.shape[0]
     fetches = [pltpu.make_async_copy(error.at[i], e_all.at[i], e_sem.at[i]) for i in range(blocks)]
-    first = pltpu.make_async_copy(hid_in, hid, h_sem)
-    for copy in [first] + fetches:
+    for copy in fetches:
         copy.start()
     turned[...] = total[...].T[: turned.shape[0]]
     puts = []
-    first.wait()
     for i in range(blocks):
         fetches[i].wait()
         g = jnp.dot(hid[...], e_all[i], preferred_element_type=F32).astype(BF)
@@ -561,13 +602,11 @@
             jax.ShapeDtypeStruct((units, blocks * WIDTH, LANES), BF),
             jax.ShapeDtypeStruct((keep, 8), F32),
         ),
-        in_specs=[hbm, vmem, hbm],
+        in_specs=[vmem, vmem, hbm],
         out_specs=(hbm, vmem),
         scratch_shapes=[
-            pltpu.VMEM(hid.shape, BF),
             pltpu.VMEM(error.shape, BF),
             pltpu.VMEM((blocks, units, WIDTH, LANES), BF),
-            pltpu.SemaphoreType.DMA,
             pltpu.SemaphoreType.DMA((blocks,)),
             pltpu.SemaphoreType.DMA((blocks,)),
         ],

time: 64.5 us -> 68.9 us (1.068)
  Pallas kernels: 63.7 us -> 68 us
    pallas_call x1, Pallas kernels: 54.7 us -> 59.8 us  [forward(): pl.pallas_call(functools.partial(forward_kernel, n_run, n_strip), out_sha...]
    pallas_call x1, Pallas kernels: 8.97 us -> 8.23 us  [output_gradient(): pl.pallas_call(output_kernel, out_shape=(jax.ShapeDtypeStruct((units, blo...]
where the time goes in v4:
time: 68.9 us; the launch traced here: 68.7 us
  Pallas kernels  68 us (99%)
    pallas_call x1, Pallas kernels, forward(): pl.pallas_call(functools.partial(forward_kernel, n_run, n_strip), out_sha...  59.8 us
    pallas_call x1, Pallas kernels, output_gradient(): pl.pallas_call(output_kernel, out_shape=(jax.ShapeDtypeStruct((units, blo...  8.23 us

profile of v4, /device:TPU:1, one launch (start us, length us, event | category | flops | bytes accessed | tf_op | source)
XLA Modules:
  0.0 68.7 jit_solution(15922721704558874550)
XLA Ops:
  0.6 59.8 %forward.1 = (bf16[8,256,1024]{2,1,0:T(8,128)(2,1)}, bf16[512,256]{1,0:T(8,128)(2,1)}, f32[8,128]{1,0:T(8,128)}) custom-call(f32[6,8]{1,0:T(8,128)} %levels_in.1, s32[6,64]{1,0:T(8,128)} %bitcast.2, f32[8,512]{1,0:T(8,128)} %w_in_in.1, f32[64,8,256]{2,1,0:T(8,128)} %base.1, s32[64,8,256]{2,1,0:T(8,128)} %material.1, bf16[512,64,128]{2,1,0:T(8,128)(2,1)} %weight.1), custom_call_target="tpu_custom_call" | custom-call | tf_op jit(solution)/shard_map/forward/pallas_call | solution.py:542
  60.5 8.2 %output_gradient.1 = (bf16[512,64,128]{2,1,0:T(8,128)(2,1)}, f32[4,8]{1,0:T(4,128)}) custom-call(bf16[512,256]{1,0:T(8,128)(2,1)} %get-tuple-element.7.hid, f32[8,128]{1,0:T(8,128)} %get-tuple-element.8.total, bf16[8,256,1024]{2,1,0:T(8,128)(2,1)} %get-tuple-element.9.error), custom_call_target="tpu_custom_call" | custom-call | tf_op jit(solution)/shard_map/output_gradient/pallas_call | solution.py:599

commit v5 on v3

--- a/solution.py
+++ b/solution.py
@@ -17,6 +17,7 @@
 CHUNK = 35
 WIDTH = 8
 TURN = 2
+AHEAD = 3
 
 
 def run_values(levels_ref, index_ref):
@@ -101,13 +102,13 @@
     for where in peers:
         pl.semaphore_signal(barrier, inc=1, device_id=where, device_id_type=MESH)
     halos = []
-    for i, (src, dst) in enumerate(((base, bx), (material, mx))):
+    for i, dst in enumerate((bx, mx)):
         for j, (first, to, target) in enumerate(
-            ((rows_x - STEPS, 0, right), (0, STEPS + rows_x, left))
+            ((rows_x, 0, right), (STEPS, STEPS + rows_x, left))
         ):
             halos.append(
                 pltpu.make_async_remote_copy(
-                    src_ref=src.at[pl.ds(first, STEPS)],
+                    src_ref=dst.at[pl.ds(first, STEPS)],
                     dst_ref=dst.at[pl.ds(to, STEPS)],
                     send_sem=halo_send.at[2 * i + j],
                     recv_sem=halo_recv.at[2 * i + j],
@@ -526,17 +527,21 @@
     )(levels, index, w_in, base, material, weight)
 
 
-def output_kernel(hid_in, total, error, grad, turned, hid, e_all, g_all, h_sem, e_sem, g_sem):
+def output_kernel(
+    hid_in, total_in, error, grad, turned, hid, total, e_all, g_all, h_sem, t_sem, e_sem, g_sem
+):
     blocks = e_all.shape[0]
     fetches = [pltpu.make_async_copy(error.at[i], e_all.at[i], e_sem.at[i]) for i in range(blocks)]
     first = pltpu.make_async_copy(hid_in, hid, h_sem)
-    for copy in [first] + fetches:
+    second = pltpu.make_async_copy(total_in, total, t_sem)
+    for copy in [first, *fetches[:AHEAD], second]:
         copy.start()
-    turned[...] = total[...].T[: turned.shape[0]]
     puts = []
     first.wait()
     for i in range(blocks):
         fetches[i].wait()
+        if i + AHEAD < blocks:
+            fetches[i + AHEAD].start()
         g = jnp.dot(hid[...], e_all[i], preferred_element_type=F32).astype(BF)
         g = jnp.stack([g[:, x * LANES : (x + 1) * LANES] for x in range(WIDTH)], axis=0)
         g_all[i] = jnp.swapaxes(g, 0, 1)
@@ -546,6 +551,8 @@
             )
         )
         puts[-1].start()
+    second.wait()
+    turned[...] = total[...].T[: turned.shape[0]]
     for copy in puts:
         copy.wait()
 
@@ -561,12 +568,14 @@
             jax.ShapeDtypeStruct((units, blocks * WIDTH, LANES), BF),
             jax.ShapeDtypeStruct((keep, 8), F32),
         ),
-        in_specs=[hbm, vmem, hbm],
+        in_specs=[hbm, hbm, hbm],
         out_specs=(hbm, vmem),
         scratch_shapes=[
             pltpu.VMEM(hid.shape, BF),
+            pltpu.VMEM(total.shape, F32),
             pltpu.VMEM(error.shape, BF),
             pltpu.VMEM((blocks, units, WIDTH, LANES), BF),
+            pltpu.SemaphoreType.DMA,
             pltpu.SemaphoreType.DMA,
             pltpu.SemaphoreType.DMA((blocks,)),
             pltpu.SemaphoreType.DMA((blocks,)),

time: 64.5 us -> 62.8 us (0.974)
  Pallas kernels: 63.7 us -> 62 us
    pallas_call x1, Pallas kernels: 8.97 us -> 7.53 us  [output_gradient(): pl.pallas_call(output_kernel, out_shape=(jax.ShapeDtypeStruct((units, blo...]
where the time goes in v5:
time: 62.8 us; the launch traced here: 62.7 us
  Pallas kernels  62 us (99%)
  between operations  0.64 us (1%)
    pallas_call x1, Pallas kernels, forward(): pl.pallas_call(functools.partial(forward_kernel, n_run, n_strip), out_sha...  54.5 us
    pallas_call x1, Pallas kernels, output_gradient(): pl.pallas_call(output_kernel, out_shape=(jax.ShapeDtypeStruct((units, blo...  7.53 us

profile of v5, /device:TPU:1, one launch (start us, length us, event | category | flops | bytes accessed | tf_op | source)
XLA Modules:
  0.0 62.7 jit_solution(3821196100678626101)
XLA Ops:
  0.6 54.5 %forward.1 = (bf16[8,256,1024]{2,1,0:T(8,128)(2,1)}, bf16[512,256]{1,0:T(8,128)(2,1)}, f32[8,128]{1,0:T(8,128)}) custom-call(f32[6,8]{1,0:T(8,128)} %levels_in.1, s32[6,64]{1,0:T(8,128)} %bitcast.2, f32[8,512]{1,0:T(8,128)} %w_in_in.1, f32[64,8,256]{2,1,0:T(8,128)} %base.1, s32[64,8,256]{2,1,0:T(8,128)} %material.1, bf16[512,64,128]{2,1,0:T(8,128)(2,1)} %weight.1), custom_call_target="tpu_custom_call" | custom-call | tf_op jit(solution)/shard_map/forward/pallas_call | solution.py:500
  55.2 7.5 %output_gradient.1 = (bf16[512,64,128]{2,1,0:T(8,128)(2,1)}, f32[4,8]{1,0:T(4,128)}) custom-call(bf16[512,256]{1,0:T(8,128)(2,1)} %get-tuple-element.7.hid_in, f32[8,128]{1,0:T(8,128)} %get-tuple-element.8.total_in, bf16[8,256,1024]{2,1,0:T(8,128)(2,1)} %get-tuple-element.9.error), custom_call_target="tpu_custom_call" | custom-call | tf_op jit(solution)/shard_map/output_gradient/pallas_call | solution.py:565
